TPU v7x, 32 devices: a whole 2x2x4 slice. The times are simulated.
32 devices in a mesh: parts: 32 (over z, y, x, core).
Axes of the slice: x: 2, y: 2, z: 4, core: 2. Of those that a mesh axis runs over, the one named last changes fastest.
Arguments:
- rhs: float32 [216, 16384], P(None, 'parts'), may hold values from -60 to 90
- start: float32 [216, 16384], P(None, 'parts'), may hold values from -3.75 to 5.625
- spectrum_top: float32 [1], replicated, may hold values from 10 to 20
- elem_code: int32 [16384], P('parts'), may hold values from 0 to 2, as said below
- rec_elem: int32 [98304], P('parts'), may hold values from 0 to 511, as said below
- rec_dir: int32 [98304], P('parts'), may hold values from 0 to 5
- rec_sub: int32 [98304], P('parts'), may hold values from 0 to 5, as said below
- rec_peer: int32 [98304], P('parts'), may hold values from -1 to 31, as said below
- rec_index: int32 [98304], P('parts'), may hold values from 0 to 3071, as said below
- send_rec: int32 [262144], P('parts'), may hold values from 0 to 3071, as said below
Outputs:
- solution: float32 [216, 16384], P(None, 'parts')
- norms: float32 [3, 2], replicated
Inputs may be any that keep to these rules, and one draw needn't show every extreme that they name: `elem_code`: 0 marks an empty slot, 1 a fine element, 2 a coarse element; a device's live slots come first. `rec_elem`: always a live element of the record's device. `rec_sub`: 0 to 3: a quarter of a coarse face facing a fine element; 4: the whole face; 5: an unused slot, which comes after the device's used records. `rec_peer`: -1 at the channel's ends and on unused slots. A partner is never more than 7 devices away; its face has the opposite direction, and the partner's partner is the record itself. `rec_index`: A record index on the same device, or a slot of the partner device's send list to this device. `send_rec`: entries of slots that no record names are arbitrary. At most 256 slots are named from one device to another, and some pair of devices uses all 256.
All inputs are finite; a program needn't handle non-finite values.
Results may differ from a plain program's by a relative error of at most 0.0003.
Values sent between devices are 32-bit elements; how exact they have to be, the bound alone decides.
A program may use at most 128 MiB of HBM per device.

v0:
```python
import functools
import math

import jax
import jax.numpy as jnp
import numpy as np
from jax import lax
from jax.experimental import pallas as pl
from jax.experimental.pallas import tpu as pltpu
from jax.sharding import PartitionSpec as P

LD = 4
ITERS = 3


PENALTY = 36.0
BOTTOM_RATIO = 8.0


def lobatto_tables():
    root_seven = math.sqrt(7.0)
    inner_root = math.sqrt(1.0 / 3.0 - 2.0 * root_seven / 21.0)
    outer_root = math.sqrt(1.0 / 3.0 + 2.0 * root_seven / 21.0)
    points = (np.array([-1.0, -outer_root, -inner_root, inner_root, outer_root, 1.0]) + 1.0) / 2.0
    weights = (
        np.array(
            [
                1.0 / 15.0,
                (14.0 - root_seven) / 30.0,
                (14.0 + root_seven) / 30.0,
                (14.0 + root_seven) / 30.0,
                (14.0 - root_seven) / 30.0,
                1.0 / 15.0,
            ]
        )
        / 2.0
    )
    barycentric = np.array(
        [1.0 / np.prod([points[j] - points[k] for k in range(6) if k != j]) for j in range(6)]
    )
    derivative = np.zeros((6, 6))
    for i in range(6):
        for j in range(6):
            if i != j:
                derivative[i, j] = barycentric[j] / barycentric[i] / (points[i] - points[j])
        derivative[i, i] = -np.sum(derivative[i])
    halves = np.zeros((2, 6, 6))
    for which_half in range(2):
        targets = (points + which_half) / 2.0
        for i in range(6):
            for j in range(6):
                halves[which_half, i, j] = np.prod(
                    [(targets[i] - points[k]) / (points[j] - points[k]) for k in range(6) if k != j]
                )
    column_sums = np.sum(derivative * derivative * weights[:, None], axis=0)
    stiff_diag = (
        column_sums[:, None, None] * weights[None, :, None] * weights[None, None, :]
        + weights[:, None, None] * column_sums[None, :, None] * weights[None, None, :]
        + weights[:, None, None] * weights[None, :, None] * column_sums[None, None, :]
    )
    return (weights, derivative, halves, stiff_diag.reshape(216))


BF16 = jnp.bfloat16
F32 = jnp.float32


def split_np(matrix):
    high = np.asarray(matrix, np.float32).astype(BF16)
    low = (np.asarray(matrix, np.float64) - high.astype(np.float64)).astype(np.float32).astype(BF16)
    return high, low


def operators():
    weights, derivative, halves, stiff_diag = lobatto_tables()
    eye = np.eye(6)
    trace_rows = []
    for direction in range(6):
        axis_index = direction // 2
        layer_index = 5 * (direction % 2)
        orientation = 2.0 * (direction % 2) - 1.0
        for row in (eye[layer_index], orientation * derivative[layer_index]):
            factors = [eye, eye, eye]
            factors[axis_index] = row[None, :]
            trace_rows.append(np.kron(np.kron(factors[0], factors[1]), factors[2]))
    traces = np.concatenate(trace_rows, axis=0)
    stiff_1d = derivative.T @ (weights[:, None] * derivative)
    mass = np.diag(weights)
    stiffness = (
        np.kron(np.kron(stiff_1d, mass), mass)
        + np.kron(np.kron(mass, stiff_1d), mass)
        + np.kron(np.kron(mass, mass), stiff_1d)
    )
    blocks = []
    for sub in range(4):
        quarter = np.kron(halves[sub % 2], halves[sub // 2])
        blocks.append(np.kron(np.eye(2), quarter))
    return traces, stiffness, np.concatenate(blocks, axis=0), np.outer(weights, weights).reshape(36, 1), stiff_diag


def split(value):
    high = value.astype(BF16)
    return high, (value - high.astype(F32)).astype(BF16)


def dot(left, right):
    return jnp.dot(left, right, preferred_element_type=F32)


def dot3(left_high, left_low, right):
    high, low = split(right)
    return dot(left_high, high) + (dot(left_high, low) + dot(left_low, high))


def one_hot(index_row, rows, base=0):
    count = index_row.shape[1]
    position = lax.broadcasted_iota(jnp.int32, (rows, count), 0)
    return jnp.where(position == index_row - base, 1.0, 0.0).astype(BF16)


def pick(traces, elem, direction, sub, onto):
    wide = dot(traces, one_hot(elem, traces.shape[1]))
    face = jnp.zeros((72, elem.shape[1]), F32)
    for d in range(6):
        both = wide[72 * d : 72 * d + 72] + wide[432 + 72 * d : 432 + 72 * d + 72]
        face = jnp.where(direction == d, both, face)
    high, low = split(face)
    quarters = dot(onto, jnp.concatenate([high, low, high], axis=0))
    result = face
    for s in range(4):
        result = jnp.where(sub == s, quarters[72 * s : 72 * s + 72], result)
    return result


def send_kernel(x_ref, inv_ref, code_ref, mat_high, mat_low, onto_ref, out_ref, traces_ref):
    @pl.when(pl.program_id(0) == 0)
    def _():
        raw = dot3(mat_high[...], mat_low[...], x_ref[...])
        row = lax.broadcasted_iota(jnp.int32, raw.shape, 0)
        raw = jnp.where(lax.rem(row, 72) >= 36, raw * inv_ref[...], raw)
        high, low = split(raw)
        traces_ref[0:432] = high
        traces_ref[432:864] = low

    code = code_ref[...]
    picked = pick(traces_ref[...], code[0:1], code[1:2], code[2:3], onto_ref[...])
    capacity = out_ref.shape[2]
    for k in range(out_ref.shape[0]):
        out_ref[k] = picked[:, k * capacity : (k + 1) * capacity]


def exchange_kernel(
    steps, axis, width, src_ref, x_ref, traces_ref, code_ref, onto_ref, stiff_high, stiff_low,
    dst_ref, own_ref, near_ref, volume_ref, send_sem, recv_sem,
):
    count = lax.axis_size(axis)
    me = lax.axis_index(axis)
    barrier = pltpu.get_barrier_semaphore()
    peers = [lax.rem(me + step + count, count) for step in steps]
    for peer in peers:
        pl.semaphore_signal(barrier, inc=1, device_id=(peer,), device_id_type=pl.DeviceIdType.MESH)
    pl.semaphore_wait(barrier, len(steps))
    copies = []
    for k, peer in enumerate(peers):
        copy = pltpu.make_async_remote_copy(
            src_ref=src_ref.at[k],
            dst_ref=dst_ref.at[k],
            send_sem=send_sem.at[k],
            recv_sem=recv_sem.at[k],
            device_id=(peer,),
            device_id_type=pl.DeviceIdType.MESH,
        )
        copy.start()
        copies.append(copy)

    def step_tile(i, carry):
        part = pl.ds(pl.multiple_of(i * width, width), width)
        code = code_ref[:, part]
        own_ref[:, part] = pick(traces_ref[...], code[0:1], code[1:2], code[2:3], onto_ref[...])
        near_ref[:, part] = pick(traces_ref[...], code[3:4], code[4:5], code[5:6], onto_ref[...])
        return carry

    lax.fori_loop(0, code_ref.shape[1] // width, step_tile, 0)
    volume_ref[...] = dot3(stiff_high[...], stiff_low[...], x_ref[...])
    for copy in copies:
        copy.wait()


def norms_kernel(axis, sums_ref, out_ref, landing, send_sem, recv_sem):
    count = lax.axis_size(axis)
    me = lax.axis_index(axis)
    barrier = pltpu.get_barrier_semaphore()

    def greet(k, carry):
        peer = lax.rem(me + k, count)
        pl.semaphore_signal(barrier, inc=1, device_id=(peer,), device_id_type=pl.DeviceIdType.MESH)
        return carry

    def copy_to(k):
        return pltpu.make_async_remote_copy(
            src_ref=sums_ref,
            dst_ref=landing.at[k],
            send_sem=send_sem.at[k],
            recv_sem=recv_sem.at[k],
            device_id=(lax.rem(me + k, count),),
            device_id_type=pl.DeviceIdType.MESH,
        )

    def start(k, carry):
        copy_to(k).start()
        return carry

    def finish(k, carry):
        copy_to(k).wait()
        return carry

    lax.fori_loop(1, count, greet, 0)
    pl.semaphore_wait(barrier, count - 1)
    lax.fori_loop(1, count, start, 0)
    landing[0] = sums_ref[...]
    lax.fori_loop(1, count, finish, 0)

    def add(j, total):
        return total + landing[lax.rem(me + count - j, count)]

    total = lax.fori_loop(0, count, add, jnp.zeros(out_ref.shape, F32))
    out_ref[...] = jnp.broadcast_to(jnp.sum(total, axis=1, keepdims=True), out_ref.shape)


def apply_kernel(
    row_index, coef_ref, x_ref, dirn_ref, rhs_ref, elem_ref, prec_ref, recv_ref, own_ref, near_ref,
    volume_ref, code_ref, rows_ref, size_ref, off_ref, weight_ref, lift_high, lift_low, prior_ref,
    x_out, dirn_out, sums_out, pool, total,
):
    peer_count = recv_ref.shape[0]

    @pl.when(pl.program_id(0) == 0)
    def _():
        for k in range(peer_count):
            high, low = split(recv_ref[k])
            pool[144 * k : 144 * k + 72] = high
            pool[144 * k + 72 : 144 * k + 144] = low
        total[...] = jnp.zeros_like(total)

    code = code_ref[...]
    direction, sub = code[1:2], code[2:3]
    bound = code[6:7] == -1
    width = sub.shape[1]
    own = own_ref[...]
    wide = dot(pool[...], one_hot(code[7:8], pool.shape[1]))
    partner = near_ref[...]
    for k in range(peer_count):
        both = wide[144 * k : 144 * k + 72] + wide[144 * k + 72 : 144 * k + 144]
        partner = jnp.where(code[6:7] == k, both, partner)
    own_value, own_slope = own[0:36], own[36:72]
    part_value = jnp.where(bound, 0.0, partner[0:36])
    part_slope = jnp.where(bound, -own_slope, partner[36:72])
    jump = own_value - part_value
    flux = 0.5 * (own_slope - part_slope)
    mortar = size_ref[0:1]
    area = mortar * mortar
    weight = weight_ref[...] * size_ref[1:2]
    term_value = weight * (PENALTY * mortar * jump - area * flux)
    term_slope = -weight * (jnp.where(bound, 1.0, 0.5) * area) * jump
    terms = jnp.concatenate([term_value, term_slope], axis=0)
    spread = jnp.concatenate([jnp.where(sub == s, terms, 0.0) for s in range(4)], axis=0)
    spread_high, spread_low = split(spread)
    back = dot(off_ref[...], jnp.concatenate([spread_high, spread_low, spread_high], axis=0))
    back = jnp.where(sub >= 4, terms, back)
    spread = jnp.concatenate([jnp.where(direction == d, back, 0.0) for d in range(6)], axis=0)
    wide_high, wide_low = split(spread)
    lanes = lax.broadcasted_iota(jnp.int32, (width, total.shape[1]), 1)
    hot = jnp.where(lanes == rows_ref[...], 1.0, 0.0).astype(BF16)
    total[...] += dot(wide_high, hot) + dot(wide_low, hot)

    @pl.when(pl.program_id(0) == pl.num_programs(0) - 1)
    def _():
        size, inv = elem_ref[0:1], elem_ref[1:2]
        field = x_ref[...]
        row = lax.broadcasted_iota(jnp.int32, total.shape, 0)
        faces = jnp.where(lax.rem(row, 72) >= 36, total[...] * inv, total[...])
        applied = size * volume_ref[...]
        applied = applied + dot3(lift_high[...], lift_low[...], faces)
        residual = jnp.where(size > 0.0, rhs_ref[...] - applied, 0.0)
        scaled = residual * (inv * prec_ref[...])
        step = coef_ref[0] * dirn_ref[...] + coef_ref[1] * scaled
        dirn_out[...] = step
        x_out[...] = field + step
        squares = jnp.sum(residual * residual, axis=0, keepdims=True)
        products = jnp.sum(residual * scaled, axis=0, keepdims=True)
        fold = lambda line: sum(line[:, k : k + 128] for k in range(0, line.shape[1], 128))
        row = lax.broadcasted_iota(jnp.int32, sums_out.shape, 0)
        later = jnp.where(row == 2 * row_index + 1, fold(products), prior_ref[...])
        sums_out[...] = jnp.where(row == 2 * row_index, fold(squares), later)


def take_small(tables, index):
    rows = tables.shape[1] // 128
    fine = (jnp.arange(128, dtype=jnp.int32)[:, None] == (index % 128)[None, :]).astype(BF16)
    wide = jnp.dot(tables.reshape(-1, 128).astype(BF16), fine, preferred_element_type=F32)
    wide = wide.reshape(tables.shape[0], rows, -1)
    coarse = jnp.arange(rows, dtype=jnp.int32)[:, None] == (index // 128)[None, :]
    return jnp.sum(jnp.where(coarse[None], wide, 0.0), axis=1).astype(jnp.int32)


def tile(count):
    for width in (512, 256, 128):
        if count % width == 0:
            return width
    return count


def whole(shape):
    return pl.BlockSpec(shape, lambda i: (0,) * len(shape))


def on_device(
    rhs, start, spectrum_top, elem_code, rec_elem, rec_dir, rec_sub, rec_peer, rec_index, send_rec
):
    traces, stiffness, interp, face_weight, stiff_diag = operators()
    part_count = lax.axis_size("parts")
    own_index = lax.axis_index("parts")
    elem_count = rhs.shape[1]
    record_count = rec_elem.shape[0]
    capacity = send_rec.shape[0] // part_count
    far_reach = 2 * LD - 1
    code_float = elem_code.astype(F32)
    elem_size = 0.5 * code_float
    inv_size = jnp.where(elem_code > 0, 2.0 / jnp.maximum(code_float, 1.0), 0.0)
    elem_rows = jnp.stack([elem_size, inv_size])
    is_bound = rec_peer < 0
    is_local = rec_peer == own_index
    is_remote = jnp.logical_and(jnp.logical_not(is_bound), jnp.logical_not(is_local))
    offset = own_index - rec_peer
    position = jnp.where(offset < 0, offset + far_reach, offset + far_reach - 1)
    block = jnp.where(is_remote, position, jnp.where(is_bound, -1, -2))
    steps = list(range(-far_reach, 0)) + list(range(1, far_reach + 1))
    lists = send_rec.reshape(part_count, capacity)
    lists = jnp.concatenate([lists[part_count - far_reach :], lists, lists[:far_reach]], axis=0)
    lists = lax.dynamic_slice_in_dim(lists, own_index, 2 * far_reach + 1, 0)
    send_cols = jnp.concatenate([lists[:far_reach], lists[far_reach + 1 :]], axis=0).reshape(-1)
    send_count = send_cols.shape[0]

    own_size = 0.5 * take_small(elem_code[None], rec_elem)[0].astype(F32)
    mortar_size = jnp.where(rec_sub < 4, 0.5 * own_size, own_size)
    size_rows = jnp.stack([mortar_size, (rec_sub < 5).astype(F32)])
    tables = jnp.stack([rec_elem // 256, rec_elem % 256, rec_dir * 8 + rec_sub])
    found = take_small(tables, jnp.concatenate([send_cols, rec_index]))
    found = jnp.stack([found[0] * 256 + found[1], found[2] // 8, found[2] % 8])
    send_code = found[:, :send_count]
    near = jnp.where(is_local[None], found[:, send_count:], -1)
    rec_code = jnp.concatenate(
        [jnp.stack([rec_elem, rec_dir, rec_sub]), near, block[None], rec_index[None]],
        axis=0,
    )
    rec_rows = rec_elem[:, None]

    mat_high, mat_low = split_np(traces)
    lift_high, lift_low = split_np(traces.T)
    stiff_high, stiff_low = split_np(stiffness)
    onto_high, onto_low = split_np(interp)
    onto = np.concatenate([onto_high, onto_high, onto_low], axis=1)
    flat = np.concatenate([interp[72 * s : 72 * s + 72].T for s in range(4)], axis=1)
    off_high, off_low = split_np(flat)
    off = np.concatenate([off_high, off_high, off_low], axis=1)
    prec = jnp.asarray((1.0 / stiff_diag).reshape(216, 1), F32)
    weight = jnp.asarray(face_weight, F32)

    send_tile, rec_tile, peer_count = 2 * capacity, tile(record_count), len(steps)
    params = pltpu.CompilerParams(vmem_limit_bytes=60 * 1024 * 1024)
    field = (216, elem_count)

    def send_call(x):
        return pl.pallas_call(
            send_kernel,
            grid=(send_count // send_tile,),
            in_specs=[
                whole(field),
                whole((1, elem_count)),
                pl.BlockSpec((3, send_tile), lambda i: (0, i)),
                whole((432, 216)),
                whole((432, 216)),
                whole((288, 216)),
            ],
            out_specs=[pl.BlockSpec((2, 72, capacity), lambda i: (i, 0, 0)), whole((864, elem_count))],
            out_shape=[
                jax.ShapeDtypeStruct((peer_count, 72, capacity), F32),
                jax.ShapeDtypeStruct((864, elem_count), BF16),
            ],
            compiler_params=params,
            name="send_traces",
        )(x, inv_size[None], send_code, jnp.asarray(mat_high), jnp.asarray(mat_low), jnp.asarray(onto))

    vmem = pl.BlockSpec(memory_space=pltpu.VMEM)

    def exchange(outgoing, x, element_traces):
        return pl.pallas_call(
            functools.partial(exchange_kernel, steps, "parts", rec_tile),
            in_specs=[pl.BlockSpec(memory_space=pl.ANY)] + [vmem] * 6,
            out_specs=[pl.BlockSpec(memory_space=pl.ANY)] + [vmem] * 3,
            out_shape=[
                jax.ShapeDtypeStruct((peer_count, 72, capacity), F32),
                jax.ShapeDtypeStruct((72, record_count), F32),
                jax.ShapeDtypeStruct((72, record_count), F32),
                jax.ShapeDtypeStruct(field, F32),
            ],
            scratch_shapes=[
                pltpu.SemaphoreType.DMA((peer_count,)),
                pltpu.SemaphoreType.DMA((peer_count,)),
            ],
            compiler_params=pltpu.CompilerParams(
                collective_id=0, has_side_effects=True, vmem_limit_bytes=60 * 1024 * 1024
            ),
            name="exchange",
        )(
            outgoing, x, element_traces, rec_code, jnp.asarray(onto),
            jnp.asarray(stiff_high), jnp.asarray(stiff_low),
        )

    def all_sums(sums):
        return pl.pallas_call(
            functools.partial(norms_kernel, "parts"),
            in_specs=[vmem],
            out_specs=vmem,
            out_shape=jax.ShapeDtypeStruct((8, 128), F32),
            scratch_shapes=[
                pltpu.VMEM((part_count, 8, 128), F32),
                pltpu.SemaphoreType.DMA((part_count,)),
                pltpu.SemaphoreType.DMA((part_count,)),
            ],
            compiler_params=pltpu.CompilerParams(collective_id=1, has_side_effects=True),
            name="all_sums",
        )(sums)

    def apply_call(row_index, coef, x, dirn, received, own, near_traces, volume, sums):
        tiles = lambda rows: pl.BlockSpec((rows, rec_tile), lambda i: (0, i))
        return pl.pallas_call(
            functools.partial(apply_kernel, row_index),
            grid=(record_count // rec_tile,),
            in_specs=[
                pl.BlockSpec(memory_space=pltpu.SMEM),
                whole(field),
                whole(field),
                whole(field),
                whole((2, elem_count)),
                whole((216, 1)),
                whole((peer_count, 72, capacity)),
                tiles(72),
                tiles(72),
                whole(field),
                tiles(8),
                pl.BlockSpec((rec_tile, 1), lambda i: (i, 0)),
                tiles(2),
                whole((72, 864)),
                whole((36, 1)),
                whole((216, 432)),
                whole((216, 432)),
                whole((8, 128)),
            ],
            out_specs=[whole(field), whole(field), whole((8, 128))],
            out_shape=[
                jax.ShapeDtypeStruct(field, F32),
                jax.ShapeDtypeStruct(field, F32),
                jax.ShapeDtypeStruct((8, 128), F32),
            ],
            scratch_shapes=[
                pltpu.VMEM((144 * peer_count, capacity), BF16),
                pltpu.VMEM((432, elem_count), F32),
            ],
            compiler_params=params,
            name="apply_operator",
        )(
            coef, x, dirn, rhs, elem_rows, prec, received, own, near_traces, volume, rec_code, rec_rows,
            size_rows, jnp.asarray(off), weight, jnp.asarray(lift_high), jnp.asarray(lift_low), sums,
        )

    scale_total = 216.0 * elem_count * part_count
    top_value = spectrum_top[0]
    bottom = top_value / BOTTOM_RATIO
    center = 0.5 * (top_value + bottom)
    radius = 0.5 * (top_value - bottom)
    sigma_ratio = center / radius
    rho_prev = 1.0 / sigma_ratio
    coef = jnp.stack([jnp.zeros_like(center), 1.0 / center])
    x, dirn, sums = start, start, jnp.zeros((8, 128), F32)
    for step_index in range(ITERS):
        if step_index:
            rho_next = 1.0 / (2.0 * sigma_ratio - rho_prev)
            coef = jnp.stack([rho_next * rho_prev, 2.0 * rho_next / radius])
            rho_prev = rho_next
        outgoing, element_traces = send_call(x)
        moved = exchange(outgoing, x, element_traces)
        x, dirn, sums = apply_call(step_index, coef, x, dirn, *moved, sums)
    norms = 0.5 * jnp.log(all_sums(sums)[: 2 * ITERS, 0].reshape(ITERS, 2) / scale_total)
    return (x, norms)


def solution(mesh):
    placed = (
        P(None, "parts"),
        P(None, "parts"),
        P(),
        P("parts"),
        P("parts"),
        P("parts"),
        P("parts"),
        P("parts"),
        P("parts"),
        P("parts"),
    )
    return jax.shard_map(
        on_device, mesh=mesh, in_specs=placed, out_specs=(P(None, "parts"), P()), check_vma=False
    )
```

profile of v0, /device:TPU:0, one launch (start us, length us, event | category | flops | bytes accessed | tf_op | source)
XLA Modules:
  0.0 166.9 jit_solution(2569852053616852041)
XLA Ops:
  1.6 0.6 pad_maximum_fusion.2.coef_ref
  2.2 0.6 pad_maximum_fusion.3.coef_ref
  2.8 0.7 pad_maximum_fusion.4.coef_ref
  3.5 0.7 broadcast_compare_fusion
  4.2 0.8 convert_multiply_fusion
  4.9 0.0 copy-start.2
  4.9 0.6 pad_maximum_fusion.1.elem_ref
  5.5 0.7 fusion.22
  6.3 0.7 select_select_fusion
  7.0 0.7 compare_convert_fusion
  7.7 0.7 fusion.28
  8.4 0.8 reshape.191
  9.3 0.7 constant_dynamic-update-slice_fusion
  10.0 0.7 add_select_fusion.4
  10.8 1.0 fusion.7
  11.8 0.7 multiply_select_fusion
  12.5 0.6 pad_maximum_fusion.size_ref
  13.2 0.1 iota_compare_fusion.5
  13.3 0.0 copy-start
  13.3 0.0 copy-start.1
  13.3 0.0 copy-start.3
  13.3 0.0 copy-start.4
  13.3 1.0 fusion.4
  14.3 0.0 copy-done.2
  14.4 0.2 and_select_fusion.1
  14.6 0.1 pad_add_fusion
  14.7 0.6 slice.70.code_ref
  15.4 0.0 copy-done
  15.4 0.0 copy-done.1
  15.4 0.0 copy-done.3
  15.4 0.0 copy-done.4
  15.4 0.7 concatenate.46.code_ref
  16.1 1.7 %copy.23.rows_ref = s32[3072,1]{1,0:T(8,128)} copy(s32[3072,1]{0,1:T(1,128)S(1)} %bitcast.41) | data formatting | bytes 24576 | tf_op jit(solution)/shard_map/broadcast_in_dim | solution.py:356
  17.8 8.7 %send_traces.3 = (f32[14,72,256]{2,1,0:T(8,128)}, bf16[864,512]{1,0:T(8,128)(2,1)}) custom-call(f32[216,512]{1,0:T(8,128)} %dirn_ref.1, f32[1,512]{1,0:T(1,128)} %bitcast.43, s32[3,3584]{1,0:T(4,128)} %slice.70.code_ref, bf16[432,216]{1,0:T(8,128)(2,1)} %constant.152.clone.mat_high, bf16[432,216]{1,0:T(8,128)(2,1)} %constant.153.clone.mat_low, ...), custom_call_target="tpu_custom_call" | custom-call | tf_op jit(solution)/shard_map/send_traces/pallas_call | solution.py:374
  26.5 22.3 %exchange.3 = (f32[14,72,256]{2,1,0:T(8,128)}, f32[72,3072]{1,0:T(8,128)}, f32[72,3072]{1,0:T(8,128)}, f32[216,512]{1,0:T(8,128)}) custom-call(f32[14,72,256]{2,1,0:T(8,128)} %get-tuple-element.28.src_ref, f32[216,512]{1,0:T(8,128)} %dirn_ref.1, bf16[864,512]{1,0:T(8,128)(2,1)} %get-tuple-element.29.traces_ref, s32[8,3072]{1,0:T(8,128)} %concatenate.46.code_ref, ...), custom_call_target="tpu_custom_call" | custom-call | tf_op jit(solution)/shard_map/exchange/pallas_call | solution.py:397
  48.8 0.6 broadcast_in_dim.71.prior_ref
  49.4 15.2 %apply_operator.3 = (f32[216,512]{1,0:T(8,128)}, f32[216,512]{1,0:T(8,128)}, f32[8,128]{1,0:T(8,128)}) custom-call(f32[2]{0:T(128)} %pad_maximum_fusion.4.coef_ref, f32[216,512]{1,0:T(8,128)} %dirn_ref.1, f32[216,512]{1,0:T(8,128)} %dirn_ref.1, f32[216,512]{1,0:T(8,128)} %rhs_ref.5, f32[2,512]{1,0:T(2,128)} %pad_maximum_fusion.1.elem_ref, ...), custom_call_target="tpu_custom_call" | custom-call | tf_op jit(solution)/shard_map/apply_operator/pallas_call | solution.py:437
  64.6 8.7 %send_traces.4 = (f32[14,72,256]{2,1,0:T(8,128)}, bf16[864,512]{1,0:T(8,128)(2,1)}) custom-call(f32[216,512]{1,0:T(8,128)} %get-tuple-element.34.x_ref, f32[1,512]{1,0:T(1,128)} %bitcast.44, s32[3,3584]{1,0:T(4,128)} %slice.70.code_ref, bf16[432,216]{1,0:T(8,128)(2,1)} %constant.152.clone.mat_high, bf16[432,216]{1,0:T(8,128)(2,1)} %constant.153.clone.mat_low, ...), custom_call_target="tpu_custom_call" | custom-call | tf_op jit(solution)/shard_map/send_traces/pallas_call | solution.py:374
  73.2 21.8 %exchange.4 = (f32[14,72,256]{2,1,0:T(8,128)}, f32[72,3072]{1,0:T(8,128)}, f32[72,3072]{1,0:T(8,128)}, f32[216,512]{1,0:T(8,128)}) custom-call(f32[14,72,256]{2,1,0:T(8,128)} %get-tuple-element.36.src_ref, f32[216,512]{1,0:T(8,128)} %get-tuple-element.34.x_ref, bf16[864,512]{1,0:T(8,128)(2,1)} %get-tuple-element.37.traces_ref, ...), custom_call_target="tpu_custom_call" | custom-call | tf_op jit(solution)/shard_map/exchange/pallas_call | solution.py:397
  95.0 15.3 %apply_operator.4 = (f32[216,512]{1,0:T(8,128)}, f32[216,512]{1,0:T(8,128)}, f32[8,128]{1,0:T(8,128)}) custom-call(f32[2]{0:T(128)} %pad_maximum_fusion.3.coef_ref, f32[216,512]{1,0:T(8,128)} %get-tuple-element.34.x_ref, f32[216,512]{1,0:T(8,128)} %get-tuple-element.35.dirn_ref, f32[216,512]{1,0:T(8,128)} %rhs_ref.5, f32[2,512]{1,0:T(2,128)} %pad_maximum_fusion.1.elem_ref, ...), custom_call_target="tpu_custom_call" | custom-call | tf_op jit(solution)/shard_map/apply_operator/pallas_call | solution.py:437
  110.3 8.7 %send_traces.5 = (f32[14,72,256]{2,1,0:T(8,128)}, bf16[864,512]{1,0:T(8,128)(2,1)}) custom-call(f32[216,512]{1,0:T(8,128)} %get-tuple-element.43.x_ref, f32[1,512]{1,0:T(1,128)} %bitcast.45, s32[3,3584]{1,0:T(4,128)} %slice.70.code_ref, bf16[432,216]{1,0:T(8,128)(2,1)} %constant.152.clone.mat_high, bf16[432,216]{1,0:T(8,128)(2,1)} %constant.153.clone.mat_low, ...), custom_call_target="tpu_custom_call" | custom-call | tf_op jit(solution)/shard_map/send_traces/pallas_call | solution.py:374
  119.0 20.2 %exchange.5 = (f32[14,72,256]{2,1,0:T(8,128)}, f32[72,3072]{1,0:T(8,128)}, f32[72,3072]{1,0:T(8,128)}, f32[216,512]{1,0:T(8,128)}) custom-call(f32[14,72,256]{2,1,0:T(8,128)} %get-tuple-element.45.src_ref, f32[216,512]{1,0:T(8,128)} %get-tuple-element.43.x_ref, bf16[864,512]{1,0:T(8,128)(2,1)} %get-tuple-element.46.traces_ref, ...), custom_call_target="tpu_custom_call" | custom-call | tf_op jit(solution)/shard_map/exchange/pallas_call | solution.py:397
  139.2 15.4 %apply_operator.5 = (f32[216,512]{1,0:T(8,128)}, f32[216,512]{1,0:T(8,128)}, f32[8,128]{1,0:T(8,128)}) custom-call(f32[2]{0:T(128)} %pad_maximum_fusion.2.coef_ref, f32[216,512]{1,0:T(8,128)} %get-tuple-element.43.x_ref, f32[216,512]{1,0:T(8,128)} %get-tuple-element.44.dirn_ref, f32[216,512]{1,0:T(8,128)} %rhs_ref.5, f32[2,512]{1,0:T(2,128)} %pad_maximum_fusion.1.elem_ref, ...), custom_call_target="tpu_custom_call" | custom-call | tf_op jit(solution)/shard_map/apply_operator/pallas_call | solution.py:437
  154.6 10.7 %all_sums.1 = f32[8,128]{1,0:T(8,128)} custom-call(f32[8,128]{1,0:T(8,128)} %get-tuple-element.53.sums_ref), custom_call_target="tpu_custom_call" | custom-call | tf_op jit(solution)/shard_map/all_sums/pallas_call | solution.py:421
  165.4 0.8 multiply_reduce_fusion
  166.1 0.1 mul.69
  166.2 0.7 copy.26
  (12 shorter events, 0.2 us)
Async XLA Ops:
  4.9 9.4 %copy-start.2 = (f32[512]{0:T(512)}, f32[512]{0:T(512)S(1)}, u32[]{:S(2)}) copy-start(f32[512]{0:T(512)S(1)} %get-tuple-element.72) | copy-start | bytes 6148
  13.3 2.1 %copy-start = (s32[3072]{0:T(1024)S(1)}, s32[3072]{0:T(1024)}, u32[]{:S(2)}) copy-start(s32[3072]{0:T(1024)} %param.26) | copy-start | bytes 36868
  13.3 2.1 %copy-start.1 = (s32[3072]{0:T(1024)S(1)}, s32[3072]{0:T(1024)}, u32[]{:S(2)}) copy-start(s32[3072]{0:T(1024)} %param.24) | copy-start | bytes 36868
  13.3 2.1 %copy-start.3 = (s32[3072]{0:T(1024)S(1)}, s32[3072]{0:T(1024)}, u32[]{:S(2)}) copy-start(s32[3072]{0:T(1024)} %param.28) | copy-start | bytes 36868
  13.3 2.1 %copy-start.4 = (s32[3072]{0:T(1024)S(1)}, s32[3072]{0:T(1024)}, u32[]{:S(2)}) copy-start(s32[3072]{0:T(1024)} %param.25) | copy-start | bytes 36868
where the time goes:
time: 168 us; the launch traced here: 167 us
  Pallas kernels  147 us (88%)
  other arithmetic  9.49 us (6%)
  local copies, waits for them, and re-layouts  6.64 us (4%)
  matrix products  2.07 us (1%)
  between operations  1.78 us (1%)
    pallas_call x3, Pallas kernels, exchange(): pl.pallas_call(functools.partial(exchange_kernel, steps, 'parts', rec_til...  64.3 us
    pallas_call x3, Pallas kernels, apply_call(): pl.pallas_call(functools.partial(apply_kernel, row_index), grid=(record_c...  45.9 us
    pallas_call x3, Pallas kernels, send_call(): pl.pallas_call(send_kernel, grid=(send_count // send_tile,), in_specs=[wh...  26 us
    pallas_call x1, Pallas kernels, all_sums(): pl.pallas_call(functools.partial(norms_kernel, 'parts'), in_specs=[vmem],...  10.7 us

commit v1 on v0

--- a/solution.py
+++ b/solution.py
@@ -228,7 +228,7 @@
 
 
 def apply_kernel(
-    row_index, coef_ref, x_ref, dirn_ref, rhs_ref, elem_ref, prec_ref, recv_ref, own_ref, near_ref,
+    row_ref, coef_ref, x_ref, dirn_ref, rhs_ref, elem_ref, prec_ref, recv_ref, own_ref, near_ref,
     volume_ref, code_ref, rows_ref, size_ref, off_ref, weight_ref, lift_high, lift_low, prior_ref,
     x_out, dirn_out, sums_out, pool, total,
 ):
@@ -290,6 +290,7 @@
         products = jnp.sum(residual * scaled, axis=0, keepdims=True)
         fold = lambda line: sum(line[:, k : k + 128] for k in range(0, line.shape[1], 128))
         row = lax.broadcasted_iota(jnp.int32, sums_out.shape, 0)
+        row_index = row_ref[0]
         later = jnp.where(row == 2 * row_index + 1, fold(products), prior_ref[...])
         sums_out[...] = jnp.where(row == 2 * row_index, fold(squares), later)
 
@@ -314,7 +315,7 @@
     return pl.BlockSpec(shape, lambda i: (0,) * len(shape))
 
 
-def on_device(
+def general_path(
     rhs, start, spectrum_top, elem_code, rec_elem, rec_dir, rec_sub, rec_peer, rec_index, send_rec
 ):
     traces, stiffness, interp, face_weight, stiff_diag = operators()
@@ -435,9 +436,10 @@
     def apply_call(row_index, coef, x, dirn, received, own, near_traces, volume, sums):
         tiles = lambda rows: pl.BlockSpec((rows, rec_tile), lambda i: (0, i))
         return pl.pallas_call(
-            functools.partial(apply_kernel, row_index),
+            apply_kernel,
             grid=(record_count // rec_tile,),
             in_specs=[
+                pl.BlockSpec(memory_space=pltpu.SMEM),
                 pl.BlockSpec(memory_space=pltpu.SMEM),
                 whole(field),
                 whole(field),
@@ -470,7 +472,7 @@
             compiler_params=params,
             name="apply_operator",
         )(
-            coef, x, dirn, rhs, elem_rows, prec, received, own, near_traces, volume, rec_code, rec_rows,
+            row_index[None], coef, x, dirn, rhs, elem_rows, prec, received, own, near_traces, volume, rec_code, rec_rows,
             size_rows, jnp.asarray(off), weight, jnp.asarray(lift_high), jnp.asarray(lift_low), sums,
         )
 
@@ -481,18 +483,586 @@
     radius = 0.5 * (top_value - bottom)
     sigma_ratio = center / radius
     rho_prev = 1.0 / sigma_ratio
-    coef = jnp.stack([jnp.zeros_like(center), 1.0 / center])
-    x, dirn, sums = start, start, jnp.zeros((8, 128), F32)
-    for step_index in range(ITERS):
-        if step_index:
-            rho_next = 1.0 / (2.0 * sigma_ratio - rho_prev)
-            coef = jnp.stack([rho_next * rho_prev, 2.0 * rho_next / radius])
-            rho_prev = rho_next
+    coefs = [jnp.stack([jnp.zeros_like(center), 1.0 / center])]
+    for step_index in range(1, ITERS):
+        rho_next = 1.0 / (2.0 * sigma_ratio - rho_prev)
+        coefs.append(jnp.stack([rho_next * rho_prev, 2.0 * rho_next / radius]))
+        rho_prev = rho_next
+    coefs = jnp.stack(coefs)
+
+    def one_step(step_index, state):
+        x, dirn, sums = state
         outgoing, element_traces = send_call(x)
         moved = exchange(outgoing, x, element_traces)
-        x, dirn, sums = apply_call(step_index, coef, x, dirn, *moved, sums)
+        coef = lax.dynamic_index_in_dim(coefs, step_index, 0, False)
+        return tuple(apply_call(step_index, coef, x, dirn, *moved, sums))
+
+    x, dirn, sums = lax.fori_loop(0, ITERS, one_step, (start, start, jnp.zeros((8, 128), F32)))
     norms = 0.5 * jnp.log(all_sums(sums)[: 2 * ITERS, 0].reshape(ITERS, 2) / scale_total)
     return (x, norms)
+
+
+LATERAL = 128
+FIELDS = 9
+
+
+def iota(shape, axis):
+    return lax.broadcasted_iota(jnp.int32, shape, axis)
+
+
+def sum_rows(value):
+    return jnp.sum(value, axis=0, keepdims=True)
+
+
+def total_of(value):
+    return jnp.sum(value, axis=1, keepdims=True)
+
+
+def look_up(tables, rows, index):
+    hot = jnp.where(iota((128, index.shape[1]), 0) == (index & 127), 1.0, 0.0).astype(BF16)
+    wide = dot(tables, hot)
+    mask = iota((rows, index.shape[1]), 0) == (index >> 7)
+    count = tables.shape[0] // rows
+    return [sum_rows(jnp.where(mask, wide[k * rows : (k + 1) * rows], 0.0)) for k in range(count)]
+
+
+def regroup(columns, position, rows):
+    mask = iota((rows, position.shape[1]), 0) == (position >> 7)
+    left = jnp.concatenate([jnp.where(mask, column, 0.0) for column in columns], axis=0).astype(BF16)
+    hot = jnp.where(iota((128, position.shape[1]), 0) == (position & 127), 1.0, 0.0).astype(BF16)
+    return lax.dot_general(left, hot, (((1,), (1,)), ((), ())), preferred_element_type=F32)
+
+
+def setup_kernel(
+    axis, capacity, code_ref, elem_ref, dir_ref, sub_ref, peer_ref, index_ref,
+    code_line, elem_line, dir_line, sub_line, peer_line, index_line, lists_ref,
+    rows_ref, col_ref, send_ref, flag_ref, elem_out,
+):
+    me = lax.axis_index(axis)
+    count = lax.axis_size(axis)
+    group, place = me // LD, lax.rem(me, LD)
+    elem, direction, sub = elem_line[...], dir_line[...], sub_line[...]
+    peer, index = peer_line[...], index_line[...]
+    records, slots = elem.shape[1], code_line.shape[1]
+    chunks, table_rows, slot_rows = records // 128, records // 128, 6 * slots // 128
+    used = sub < 5
+    local = used & (peer == me)
+    bound = used & (peer < 0)
+    remote = used & (peer >= 0) & (peer != me)
+
+    kind = jnp.where(used, jnp.where(remote, direction, direction + 8), -1)
+    member = jnp.where(iota((16, records), 0) == kind, 1.0, 0.0)
+    stacked = jnp.concatenate([member[:, 128 * k : 128 * k + 128] for k in range(chunks)], axis=0)
+    upper = jnp.where(iota((128, 128), 0) < iota((128, 128), 1), 1.0, 0.0)
+    counted = dot(
+        stacked.astype(BF16), jnp.concatenate([upper, jnp.ones((128, 128), F32)], axis=1).astype(BF16)
+    )
+    carry = jnp.zeros((16, 128), F32)
+    before = []
+    for k in range(chunks):
+        before.append(counted[16 * k : 16 * k + 16, :128] + carry)
+        carry = carry + counted[16 * k : 16 * k + 16, 128:]
+    base = jnp.concatenate([jnp.zeros((8, 128), F32), carry[:8]], axis=0)
+    before = jnp.concatenate([part + base for part in before], axis=1)
+    rank = sum_rows(before * member).astype(jnp.int32)
+    in_range = used & (rank < slots)
+    slot = jnp.where(in_range, direction * slots + rank, -1)
+
+    tables = jnp.concatenate(
+        [
+            (elem_ref[...] & 127).astype(F32),
+            ((elem_ref[...] >> 7) * 8 + sub_ref[...]).astype(F32),
+            dir_ref[...].astype(F32),
+        ],
+        axis=0,
+    ).astype(BF16)
+    rows_per = capacity // 128
+    list_rows = iota(lists_ref.shape, 0)
+    lists = lists_ref[...].astype(F32)
+    channel = []
+    for d, other in ((1, group + 1), (0, group - 1)):
+        here = remote & (direction == d)
+        most = jnp.max(jnp.where(here, peer, -1), axis=1, keepdims=True)
+        least = jnp.min(jnp.where(here, peer, count), axis=1, keepdims=True)
+        wrong = here & (peer // LD != other)
+        channel.append((most, jnp.where((most >= 0) & (most != least), 1.0, 0.0), wrong))
+    wanted = []
+    for most, _, _ in channel:
+        for part in range(rows_per):
+            wanted.append(sum_rows(jnp.where(list_rows == most * rows_per + part, lists, 0.0)))
+    for pos in range(LD - 1):
+        dest = group * LD + lax.rem(place + pos + 1, LD)
+        wanted.append(sum_rows(jnp.where(list_rows == dest * rows_per, lists, 0.0)))
+    wanted.append(jnp.zeros((1, LATERAL), F32))
+    wanted = jnp.concatenate(wanted, axis=1).astype(jnp.int32)
+    wanted_count = wanted.shape[1]
+    low, high, found_dir = look_up(tables, table_rows, jnp.concatenate([wanted, index], axis=1))
+    high = high.astype(jnp.int32)
+    found_elem = low.astype(jnp.int32) + 128 * (high >> 3)
+    found_sub = high & 7
+    send_ref[0:1] = found_elem[:, :wanted_count]
+    send_ref[1:2] = found_dir[:, :wanted_count].astype(jnp.int32)
+    send_ref[2:3] = found_sub[:, :wanted_count]
+    send_ref[3:8] = jnp.zeros((5, wanted_count), jnp.int32)
+    near_elem, near_sub = found_elem[:, wanted_count:], found_sub[:, wanted_count:]
+
+    code_rows = -(-slots // 1024) * 8
+    code_table = code_ref[...].astype(F32)
+    if code_rows > code_table.shape[0]:
+        pad = jnp.zeros((code_rows - code_table.shape[0], 128), F32)
+        code_table = jnp.concatenate([code_table, pad], axis=0)
+    code = look_up(code_table.astype(BF16), code_rows, elem)[0]
+    size = 0.5 * code
+    mortar = jnp.where(sub < 4, 0.5 * size, size)
+
+    turn = lax.rem(place - lax.rem(peer, LD) + LD, LD) - 1
+    landed = jnp.where(direction < 2, index, turn * LATERAL + index)
+    split_near = jnp.where(sub < 4, sub, jnp.where(near_sub < 4, near_sub + 4, 8))
+    split_far = jnp.minimum(sub, 4)
+    real = lambda value: value.astype(F32)
+    columns = [
+        real(elem & 127),
+        real((elem >> 7) + 1),
+        real(near_elem & 127),
+        jnp.where(local, real((near_elem >> 7) + 1), 0.0),
+        jnp.where(remote, real(landed & 127), 0.0),
+        jnp.where(remote, real((landed >> 7) + 1), 0.0),
+        real(split_near),
+        real(split_far),
+        mortar,
+    ]
+    moved = regroup(columns, slot, slot_rows)
+    part = lambda k: moved[k * slot_rows : (k + 1) * slot_rows]
+    join = lambda k: jnp.where(part(k + 1) > 0.0, part(k) + 128.0 * (part(k + 1) - 1.0), -1.0)
+    own = join(0)
+    spare = col_ref.shape[1] - slot_rows
+    own_all = jnp.concatenate([own, jnp.zeros((spare, 128), F32)], axis=0)
+    col_ref[...] = jnp.transpose(own_all).astype(jnp.int32)
+    mort = part(8)
+    fields = [join(2), join(4), part(6), part(7), 36.0 * mort, 0.5 * mort * mort]
+
+    face = jnp.where(used, direction * slots + elem, -1)
+    marks = [jnp.where(used & (sub == s), 1.0, 0.0) for s in range(5)]
+    marks.append(jnp.where(bound & (sub == 4), 1.0, 0.0))
+    tally = regroup(marks, face, slot_rows)
+    fields += [tally[k * slot_rows : (k + 1) * slot_rows] for k in range(6)]
+    per = slots // 128
+    lines = []
+    for value in fields:
+        pieces = []
+        for d in range(6):
+            pieces.append(
+                jnp.concatenate([value[per * d + q : per * d + q + 1] for q in range(per)], axis=1)
+            )
+        pieces.append(jnp.zeros((2, slots), F32))
+        lines.append(jnp.concatenate(pieces, axis=0))
+    code_all = code_line[...].astype(F32)
+    size_all = 0.5 * code_all
+    inv_all = jnp.where(code_all > 0.0, 2.0 / jnp.maximum(code_all, 1.0), 0.0)
+    elem_out[0:1] = size_all
+    elem_out[1:2] = inv_all
+    elem_out[2:8] = jnp.zeros((6, slots), F32)
+    half = 0.5 * size_all
+    counts, bounds = lines[6:11], lines[11]
+    lines = lines[:6]
+    for s in range(5):
+        lines.append(36.0 * (half if s < 4 else size_all) * counts[s])
+    for s in range(4):
+        lines.append(half * half * (0.5 * counts[s]))
+    lines.append(size_all * size_all * (0.5 * (counts[4] + bounds)))
+    for k, line in enumerate(lines):
+        rows_ref[8 * k : 8 * k + 8] = line
+    rows_ref[8 * len(lines) :] = jnp.zeros((rows_ref.shape[0] - 8 * len(lines), slots), F32)
+
+    wrong = jnp.where(remote & (direction >= 2) & ((peer // LD != group) | (index >= LATERAL)), 1.0, 0.0)
+    wrong = wrong + jnp.where(bound & (sub < 4), 1.0, 0.0)
+    wrong = wrong + jnp.where(local & (sub < 4) & (near_sub < 4), 1.0, 0.0)
+    wrong = wrong + jnp.where(used & (rank >= slots), 1.0, 0.0)
+    for _, _, off in channel:
+        wrong = wrong + jnp.where(off, 1.0, 0.0)
+    faults = total_of(wrong) + channel[0][1] + channel[1][1]
+    row = iota((8, 128), 0)
+    allowed = jnp.where(row < 2, float(capacity), float(LATERAL))
+    over = jnp.where((row < 6) & (carry[:8] > allowed), 1.0, 0.0)
+    faults = faults + total_of(sum_rows(over))
+    turns = [
+        lax.rem(place - lax.rem(jnp.maximum(most, 0), LD) + LD, LD).astype(F32) for most, _, _ in channel
+    ]
+    flags = jnp.where(row == 0, faults, jnp.where(row == 1, turns[1], turns[0]))
+    flag_ref[...] = flags
+
+
+def stack2(value):
+    high = value.astype(BF16).astype(F32)
+    return jnp.concatenate([high, value - high], axis=0).astype(BF16)
+
+
+def stack3(value):
+    high = value.astype(BF16).astype(F32)
+    return jnp.concatenate([high, value - high, high], axis=0).astype(BF16)
+
+
+def fold_pair(value):
+    half = value.shape[0] // 2
+    return value[:half] + value[half:]
+
+
+def choose(blocks, rows, code):
+    last = blocks.shape[0] // rows - 1
+    result = blocks[last * rows :]
+    for q in range(last):
+        result = jnp.where(code == q, blocks[q * rows : q * rows + rows], result)
+    return result
+
+
+def main_kernel(
+    axis, iters, capacity,
+    x_ref, rhs_ref, top_ref, rows_ref, col_ref, send_ref, flag_ref, elem_ref, prec_ref,
+    trace_high, trace_low, stiff_high, stiff_low, lift_high, lift_low, onto_ref, own_ref, near_ref, far_ref,
+    x_out, norm_out,
+    dirn, volume, traces, pairs, faces, scatter, gather, gather_chan, gather_lat, send_chan, send_lat,
+    far_rows, coefs, snd_chan, snd_lat, rcv_chan, rcv_lat, sums, landing,
+    send_sem, recv_sem, sum_send, sum_recv,
+):
+    count = lax.axis_size(axis)
+    me = lax.axis_index(axis)
+    group, place = me // LD, lax.rem(me, LD)
+    groups = count // LD
+    slots = x_ref.shape[1]
+    mesh_id = pl.DeviceIdType.MESH
+    barrier = pltpu.get_barrier_semaphore()
+
+    def greet(k, carry):
+        peer = lax.rem(me + k, count)
+        pl.semaphore_signal(barrier, inc=1, device_id=(peer,), device_id_type=mesh_id)
+        return carry
+
+    lax.fori_loop(1, count, greet, 0)
+
+    def hot(mask):
+        return jnp.where(mask, 1.0, 0.0).astype(BF16)
+
+    per = slots // 128
+    columns = col_ref[...]
+    for d in range(6):
+        line = rows_ref[d : d + 1].astype(jnp.int32)
+        gather[d] = hot(iota((slots, slots), 0) == line)
+        for q in range(per):
+            column = columns[:, per * d + q : per * d + q + 1]
+            scatter[d, 128 * q : 128 * q + 128] = hot(iota((128, slots), 1) == column)
+        line = rows_ref[8 + d : 9 + d].astype(jnp.int32)
+        if d < 2:
+            gather_chan[d] = hot(iota((capacity, capacity), 0) == line[:, :capacity])
+        else:
+            gather_lat[d - 2] = hot(iota((LD * LATERAL, LATERAL), 0) == line[:, :LATERAL])
+    send_elem = send_ref[0:1]
+    send_chan[0] = hot(iota((slots, capacity), 0) == send_elem[:, :capacity])
+    send_chan[1] = hot(iota((slots, capacity), 0) == send_elem[:, capacity : 2 * capacity])
+    send_lat[...] = hot(iota((slots, LD * LATERAL), 0) == send_elem[:, 2 * capacity :])
+    chosen = jnp.zeros(far_rows.shape, F32)
+    for k, field in enumerate((3, 4, 5)):
+        block = rows_ref[8 * field : 8 * field + 8]
+        pieces = []
+        for d in range(6):
+            part = block[:, : capacity if d < 2 else LATERAL]
+            pieces.append(sum_rows(jnp.where(iota(part.shape, 0) == d, part, 0.0)))
+        chosen = jnp.where(iota(chosen.shape, 0) == k, jnp.concatenate(pieces, axis=1), chosen)
+    far_rows[...] = chosen
+
+    line = jnp.ones((1, 128), F32)
+    top = top_ref[0] * line
+    bottom = top / BOTTOM_RATIO
+    center = 0.5 * (top + bottom)
+    radius = 0.5 * (top - bottom)
+    sigma = center / radius
+    rho = 1.0 / sigma
+    coefs[0:1] = 0.0 * line
+    coefs[1:2] = 1.0 / center
+    for k in range(1, iters):
+        rho_next = 1.0 / (2.0 * sigma - rho)
+        coefs[2 * k : 2 * k + 1] = rho_next * rho
+        coefs[2 * k + 1 : 2 * k + 2] = 2.0 * rho_next / radius
+        rho = rho_next
+    x_out[...] = x_ref[...]
+    dirn[...] = jnp.zeros_like(dirn)
+    sums[...] = jnp.where(iota(sums.shape, 0) == 2 * iters, flag_ref[0:1], 0.0) * jnp.where(
+        iota(sums.shape, 1) == 0, 1.0, 0.0
+    )
+
+    size, inv = elem_ref[0:1], elem_ref[1:2]
+    pl.semaphore_wait(barrier, count - 1)
+
+    def step(it, carry):
+        field = x_out[...]
+        raw = dot3(trace_high[...], trace_low[...], field)
+        raw = jnp.where(lax.rem(iota(raw.shape, 0), 72) >= 36, raw * inv, raw)
+        traces[...] = raw
+        for d in range(6):
+            pairs[d] = stack2(raw[72 * d : 72 * d + 72])
+
+        send_dir = send_ref[1:2, 2 * capacity :]
+        lateral = jnp.zeros((72, LD * LATERAL), F32)
+        for d in range(2, 6):
+            lateral = jnp.where(send_dir == d, fold_pair(dot(pairs[d], send_lat[...])), lateral)
+        outgoing = jnp.concatenate(
+            [fold_pair(dot(pairs[1], send_chan[0])), fold_pair(dot(pairs[0], send_chan[1])), lateral], axis=1
+        )
+        outgoing = choose(dot(onto_ref[...], stack3(outgoing)), 72, send_ref[2:3])
+        snd_chan[0] = outgoing[:, :capacity]
+        snd_chan[1] = outgoing[:, capacity : 2 * capacity]
+        for pos in range(LD - 1):
+            start = 2 * capacity + pos * LATERAL
+            snd_lat[pos] = outgoing[:, start : start + LATERAL]
+
+        copies = []
+        for side in range(2):
+            other = lax.rem(group + (1 if side == 0 else groups - 1), groups)
+            for turn in range(LD):
+                k = side * LD + turn
+                copies.append(
+                    pltpu.make_async_remote_copy(
+                        src_ref=snd_chan.at[side],
+                        dst_ref=rcv_chan.at[it, side, turn],
+                        send_sem=send_sem.at[it, k],
+                        recv_sem=recv_sem.at[it, k],
+                        device_id=(other * LD + lax.rem(place + turn, LD),),
+                        device_id_type=mesh_id,
+                    )
+                )
+        for pos in range(LD - 1):
+            k = 2 * LD + pos
+            copies.append(
+                pltpu.make_async_remote_copy(
+                    src_ref=snd_lat.at[pos],
+                    dst_ref=rcv_lat.at[it, pos],
+                    send_sem=send_sem.at[it, k],
+                    recv_sem=recv_sem.at[it, k],
+                    device_id=(group * LD + lax.rem(place + pos + 1, LD),),
+                    device_id_type=mesh_id,
+                )
+            )
+        for copy in copies:
+            copy.start()
+
+        volume[...] = dot3(stiff_high[...], stiff_low[...], field) * size
+
+        def local_faces(d, inner):
+            line = lambda k: rows_ref[pl.ds(8 * k + d, 1)]
+            mass = dot(own_ref[...], stack3(traces[pl.ds(pl.multiple_of(72 * d, 8), 72)]))
+            value = jnp.zeros((40, slots), F32)
+            slope = jnp.zeros((40, slots), F32)
+            for s in range(5):
+                mass_value, mass_slope = mass[80 * s : 80 * s + 40], mass[80 * s + 40 : 80 * s + 80]
+                flux = line(11 + s)
+                value = value + (line(6 + s) * mass_value - flux * mass_slope)
+                slope = slope - flux * mass_value
+            facing = d + 1 - 2 * lax.rem(d, 2)
+            found = fold_pair(dot(pairs[facing], gather[d]))
+            found = choose(dot(near_ref[...], stack3(found)), 80, line(2).astype(jnp.int32))
+            jump, flux = line(4), line(5)
+            terms = jnp.concatenate([flux * found[40:] - jump * found[:40], flux * found[:40]], axis=0)
+            back = fold_pair(dot(stack2(terms), scatter[d]))
+            faces[pl.ds(pl.multiple_of(80 * d, 8), 80)] = back + jnp.concatenate([value, slope], axis=0)
+            return inner
+
+        lax.fori_loop(0, 6, local_faces, 0)
+        for copy in copies:
+            copy.wait()
+
+        pieces = []
+        for side in range(2):
+            turn = flag_ref[side + 1 : side + 2, 0:1]
+            got = rcv_chan[it, side, 0]
+            for k in range(1, LD):
+                got = jnp.where(turn == float(k), rcv_chan[it, side, k], got)
+            pieces.append(fold_pair(dot(stack2(got), gather_chan[side])))
+        sides = [rcv_lat[it, pos] for pos in range(LD - 1)] + [jnp.zeros((72, LATERAL), F32)]
+        got = stack2(jnp.concatenate(sides, axis=1))
+        for d in range(4):
+            pieces.append(fold_pair(dot(got, gather_lat[d])))
+        found = jnp.concatenate(pieces, axis=1)
+        found = choose(dot(far_ref[...], stack3(found)), 80, far_rows[0:1].astype(jnp.int32))
+        jump, flux = far_rows[1:2], far_rows[2:3]
+        terms = stack2(
+            jnp.concatenate([flux * found[40:] - jump * found[:40], flux * found[:40]], axis=0)
+        )
+        for d in range(6):
+            width = capacity if d < 2 else LATERAL
+            start = d * capacity if d < 2 else 2 * capacity + (d - 2) * LATERAL
+            faces[80 * d : 80 * d + 80] += fold_pair(
+                dot(terms[:, start : start + width], scatter[d, :width])
+            )
+        total = faces[...]
+        total = jnp.where(lax.rem(iota(total.shape, 0), 80) >= 40, total * inv, total)
+        applied = volume[...] + dot3(lift_high[...], lift_low[...], total)
+        residual = jnp.where(size > 0.0, rhs_ref[...] - applied, 0.0)
+        scaled = residual * (inv * prec_ref[...])
+        first = coefs[pl.ds(2 * it, 1), 0:1]
+        second = coefs[pl.ds(2 * it + 1, 1), 0:1]
+        change = first * dirn[...] + second * scaled
+        dirn[...] = change
+        x_out[...] = field + change
+        squares = sum_rows(residual * residual)
+        products = sum_rows(residual * scaled)
+        fold = lambda row: sum(row[:, k : k + 128] for k in range(0, row.shape[1], 128))
+        row = iota(sums.shape, 0)
+        kept = jnp.where(row == 2 * it + 1, fold(products), sums[...])
+        sums[...] = jnp.where(row == 2 * it, fold(squares), kept)
+        return carry
+
+    lax.fori_loop(0, iters, step, 0)
+
+    def copy_to(k):
+        return pltpu.make_async_remote_copy(
+            src_ref=sums,
+            dst_ref=landing.at[k],
+            send_sem=sum_send.at[k],
+            recv_sem=sum_recv.at[k],
+            device_id=(lax.rem(me + k, count),),
+            device_id_type=mesh_id,
+        )
+
+    def begin(k, carry):
+        copy_to(k).start()
+        return carry
+
+    def finish(k, carry):
+        copy_to(k).wait()
+        return carry
+
+    def add(j, total):
+        return total + landing[lax.rem(me + count - j, count)]
+
+    lax.fori_loop(1, count, begin, 0)
+    landing[0] = sums[...]
+    lax.fori_loop(1, count, finish, 0)
+    total = total_of(lax.fori_loop(0, count, add, jnp.zeros(sums.shape, F32)))
+    mean = total / (216.0 * slots * count)
+    logs = 0.5 * jnp.log(jnp.where(iota(total.shape, 0) < 2 * iters, mean, 1.0))
+    shown = jnp.where(iota(total.shape, 0) < 2 * iters, logs, total)
+    norm_out[...] = jnp.broadcast_to(shown, norm_out.shape)
+
+
+def wide_rows(blocks):
+    padded = []
+    for block in blocks:
+        rows = np.zeros((80, block.shape[1]))
+        rows[0:36], rows[40:76] = block[0:36], block[36:72]
+        padded.append(rows)
+    return np.concatenate(padded, axis=0)
+
+
+def three(matrix):
+    high, low = split_np(matrix)
+    return np.concatenate([high, high, low], axis=1)
+
+
+def set_up(slots, capacity, arrays, send_rec):
+    slot_rows = 6 * slots // 128
+    to_lines = lambda array: array.reshape(-1, 128)
+    to_line = lambda array: array.reshape(1, -1)
+    vmem = pl.BlockSpec(memory_space=pltpu.VMEM)
+    columns = 2 * capacity + LD * LATERAL
+    return pl.pallas_call(
+        functools.partial(setup_kernel, "parts", capacity),
+        in_specs=[vmem] * 13,
+        out_specs=[vmem] * 5,
+        out_shape=[
+            jax.ShapeDtypeStruct((136, slots), F32),
+            jax.ShapeDtypeStruct((128, 128 * -(-slot_rows // 128)), jnp.int32),
+            jax.ShapeDtypeStruct((8, columns), jnp.int32),
+            jax.ShapeDtypeStruct((8, 128), F32),
+            jax.ShapeDtypeStruct((8, slots), F32),
+        ],
+        compiler_params=pltpu.CompilerParams(vmem_limit_bytes=60 * 1024 * 1024),
+        name="set_up",
+    )(*map(to_lines, arrays), *map(to_line, arrays), to_lines(send_rec))
+
+
+def fast_path(
+    rhs, start, spectrum_top, elem_code, rec_elem, rec_dir, rec_sub, rec_peer, rec_index, send_rec
+):
+    traces, stiffness, interp, face_weight, stiff_diag = operators()
+    part_count = lax.axis_size("parts")
+    slots = rhs.shape[1]
+    capacity = send_rec.shape[0] // part_count
+    arrays = (elem_code, rec_elem, rec_dir, rec_sub, rec_peer, rec_index)
+    vmem = pl.BlockSpec(memory_space=pltpu.VMEM)
+    rows, col, send, flag, elem = set_up(slots, capacity, arrays, send_rec)
+
+    weight = np.concatenate([face_weight, face_weight], axis=0)
+    quarters = [interp[72 * s : 72 * s + 72] for s in range(4)]
+    eye = np.eye(72)
+    onto = three(np.concatenate(quarters + [eye], axis=0))
+    own = three(wide_rows([j.T @ (weight * j) for j in quarters] + [weight * eye]))
+    back = [j.T * weight.T for j in quarters]
+    near = three(wide_rows(back + [weight * j for j in quarters] + [weight * eye]))
+    far = three(wide_rows(back + [weight * eye]))
+    trace_high, trace_low = split_np(traces)
+    stiff_high, stiff_low = split_np(stiffness)
+    lift = np.zeros((216, 480))
+    for d in range(6):
+        lift[:, 80 * d : 80 * d + 36] = traces.T[:, 72 * d : 72 * d + 36]
+        lift[:, 80 * d + 40 : 80 * d + 76] = traces.T[:, 72 * d + 36 : 72 * d + 72]
+    lift_high, lift_low = split_np(lift)
+    prec = (1.0 / stiff_diag).reshape(216, 1).astype(np.float32)
+    constants = (
+        prec, trace_high, trace_low, stiff_high, stiff_low, lift_high, lift_low, onto, own, near, far
+    )
+    copies = 2 * LD + LD - 1
+    x, shown = pl.pallas_call(
+        functools.partial(main_kernel, "parts", ITERS, capacity),
+        in_specs=[vmem] * 2 + [pl.BlockSpec(memory_space=pltpu.SMEM)] + [vmem] * 16,
+        out_specs=[vmem] * 2,
+        out_shape=[jax.ShapeDtypeStruct((216, slots), F32), jax.ShapeDtypeStruct((8, 128), F32)],
+        scratch_shapes=[
+            pltpu.VMEM((216, slots), F32),
+            pltpu.VMEM((216, slots), F32),
+            pltpu.VMEM((432, slots), F32),
+            pltpu.VMEM((6, 144, slots), BF16),
+            pltpu.VMEM((480, slots), F32),
+            pltpu.VMEM((6, slots, slots), BF16),
+            pltpu.VMEM((6, slots, slots), BF16),
+            pltpu.VMEM((2, capacity, capacity), BF16),
+            pltpu.VMEM((4, LD * LATERAL, LATERAL), BF16),
+            pltpu.VMEM((2, slots, capacity), BF16),
+            pltpu.VMEM((slots, LD * LATERAL), BF16),
+            pltpu.VMEM((8, 2 * capacity + 4 * LATERAL), F32),
+            pltpu.VMEM((16, 128), F32),
+            pltpu.VMEM((2, 72, capacity), F32),
+            pltpu.VMEM((LD - 1, 72, LATERAL), F32),
+            pltpu.VMEM((ITERS, 2, LD, 72, capacity), F32),
+            pltpu.VMEM((ITERS, LD - 1, 72, LATERAL), F32),
+            pltpu.VMEM((8, 128), F32),
+            pltpu.VMEM((part_count, 8, 128), F32),
+            pltpu.SemaphoreType.DMA((ITERS, copies)),
+            pltpu.SemaphoreType.DMA((ITERS, copies)),
+            pltpu.SemaphoreType.DMA((part_count,)),
+            pltpu.SemaphoreType.DMA((part_count,)),
+        ],
+        compiler_params=pltpu.CompilerParams(
+            collective_id=2, has_side_effects=True, vmem_limit_bytes=60 * 1024 * 1024
+        ),
+        name="smooth",
+    )(
+        start, rhs, spectrum_top, rows, col, send, flag, elem, *map(jnp.asarray, constants)
+    )
+    return x, shown
+
+
+def on_device(*arguments):
+    rhs, send_rec, rec_elem = arguments[0], arguments[9], arguments[4]
+    part_count = lax.axis_size("parts")
+    capacity, slots = send_rec.shape[0] // part_count, rhs.shape[1]
+    suits = slots % 128 == 0 and rec_elem.shape[0] % 1024 == 0 and capacity % 128 == 0
+    suits = suits and capacity <= slots <= 4096 and part_count % LD == 0 and part_count >= 3 * LD
+    if not suits:
+        return general_path(*arguments)
+    x, shown = fast_path(*arguments)
+    norms = shown[: 2 * ITERS, 0].reshape(ITERS, 2)
+    return lax.cond(
+        shown[2 * ITERS, 0] > 0.0, lambda: general_path(*arguments), lambda: (x, norms)
+    )
 
 
 def solution(mesh):

time: 168 us -> 75.3 us (0.45)
  Pallas kernels: 147 us -> 70.1 us
  other arithmetic: 9.49 us -> 0 us
  local copies, waits for them, and re-layouts: 6.64 us -> 2.67 us
  matrix products: 2.07 us -> 0 us
    pallas_call x10 -> x2, Pallas kernels: 147 us -> 70.1 us  [the longest x1 66.7 us: fast_path(): pl.pallas_call(functools.partial(main_kernel, 'parts', ITERS, capacity),...]
    another operation x8 -> x0, other arithmetic: 4.63 us -> none  [the longest x2 1.34 us: on_device(): size_rows = jnp.stack([mortar_size, (rec_sub < 5).astype(F32)])]
    select_n x7 -> x0, other arithmetic: 2.45 us -> none  [the longest x2 0.76 us: take_small(): index // 128]
    broadcast_in_dim x2 -> x0, local copies, waits for them, and re-layouts: 2.27 us -> none  [the longest x1 1.68 us: on_device(): rec_rows = rec_elem[:, None]]
    dot_general x2 -> x0, matrix products: 2.07 us -> none  [take_small(): jnp.dot(tables.reshape(-1, 128).astype(BF16), fine, preferred_element_typ...]
where the time goes in v1:
time: 75.3 us; the launch traced here: 75 us
  Pallas kernels  70.1 us (93%)
  local copies, waits for them, and re-layouts  2.67 us (4%)
  between operations  2.12 us (3%)
    pallas_call x1, Pallas kernels, fast_path(): pl.pallas_call(functools.partial(main_kernel, 'parts', ITERS, capacity),...  66.7 us
    pallas_call x1, Pallas kernels, set_up(): pl.pallas_call(functools.partial(setup_kernel, 'parts', capacity), in_spe...  3.34 us
    unnamed x24, local copies, waits for them, and re-layouts  1.85 us

profile of v1, /device:TPU:0, one launch (start us, length us, event | category | flops | bytes accessed | tf_op | source)
XLA Modules:
  0.0 75.0 jit_solution(10252623592163620744)
XLA Ops:
  0.6 1.0 %copy.77.x_ref = f32[216,512]{1,0:T(8,128)S(1)} copy(f32[216,512]{1,0:T(8,128)} %param.36) | data formatting | bytes 884736
  1.6 3.3 %set_up.1 = (f32[136,512]{1,0:T(8,128)}, s32[128,128]{1,0:T(8,128)}, s32[8,1024]{1,0:T(8,128)}, f32[8,128]{1,0:T(8,128)}, f32[8,512]{1,0:T(8,128)}) custom-call(s32[4,128]{1,0:T(4,128)} %bitcast.87, s32[24,128]{1,0:T(8,128)} %bitcast.69, s32[24,128]{1,0:T(8,128)} %bitcast.77, s32[24,128]{1,0:T(8,128)} %bitcast.66, s32[24,128]{1,0:T(8,128)} %bitcast.80, ...), custom_call_target="tpu_custom_call" | custom-call | tf_op jit(solution)/shard_map/set_up/pallas_call | solution.py:966
  5.6 0.0 copy-start
  5.7 0.0 copy-start.2
  5.7 0.0 copy-start.5
  5.7 0.0 copy-start.8
  5.7 0.0 copy-start.9
  5.7 0.0 copy-start.10
  5.7 0.0 copy-start.11
  5.7 0.0 copy-start.12
  5.7 0.0 copy-start.13
  5.8 0.0 copy-start.15
  5.8 66.7 %smooth.1 = (f32[216,512]{1,0:T(8,128)S(1)}, f32[8,128]{1,0:T(8,128)S(1)}) custom-call(f32[216,512]{1,0:T(8,128)S(1)} %copy.77.x_ref, f32[216,512]{1,0:T(8,128)} %rhs_ref.1, f32[1]{0:T(128)S(6)} %copy.76.top_ref, f32[136,512]{1,0:T(8,128)} %get-tuple-element.403.rows_ref, s32[128,128]{1,0:T(8,128)} %get-tuple-element.404.col_ref, ...), custom_call_target="tpu_custom_call" | custom-call | tf_op jit(solution)/shard_map/smooth/pallas_call | solution.py:1013
  72.5 0.5 slice.60
  73.7 0.0 copy-done
  73.7 0.0 copy-done.2
  73.7 0.0 copy-done.5
  73.7 0.0 copy-done.8
  73.7 0.0 copy-done.9
  73.7 0.0 copy-done.10
  73.7 0.0 copy-done.11
  73.8 0.0 copy-done.12
  73.8 0.0 copy-done.13
  73.8 0.0 copy-done.15
  73.8 0.4 conditional.1
  73.8 0.1 copy.49
  73.9 0.1 reshape_squeeze.3
  74.0 0.1 copy.51
  74.2 0.0 copy-start.16
  74.2 0.8 %copy.81 = f32[216,512]{1,0:T(8,128)} copy(f32[216,512]{1,0:T(8,128)S(1)} %get-tuple-element.809) | data formatting | bytes 884736
  75.0 0.0 copy-done.16
  (1 shorter events, 0.0 us)
Async XLA Ops:
  5.6 68.0 %copy-start = (f32[216,512]{1,0:T(8,128)S(1)}, f32[216,512]{1,0:T(8,128)}, u32[]{:S(2)}) copy-start(f32[216,512]{1,0:T(8,128)} %rhs_ref.1) | copy-start | bytes 1327108
  5.7 68.0 %copy-start.2 = (bf16[432,216]{1,0:T(8,128)(2,1)S(1)}, bf16[432,216]{1,0:T(8,128)(2,1)}, u32[]{:S(2)}) copy-start(bf16[432,216]{1,0:T(8,128)(2,1)} %constant.190.clone.trace_high) | copy-start | bytes 559876
  5.7 68.0 %copy-start.5 = (f32[216,1]{1,0:T(8,128)S(1)}, f32[216,1]{1,0:T(8,128)}, u32[]{:S(2)}) copy-start(f32[216,1]{1,0:T(8,128)} %constant.189.clone.prec_ref) | copy-start | bytes 2596
  5.7 68.0 %copy-start.8 = (s32[3072]{0:T(1024)S(1)}, s32[3072]{0:T(1024)}, u32[]{:S(2)}) copy-start(s32[3072]{0:T(1024)} %param.41) | copy-start | bytes 36868
  5.7 68.0 %copy-start.9 = (s32[3072]{0:T(1024)S(1)}, s32[3072]{0:T(1024)}, u32[]{:S(2)}) copy-start(s32[3072]{0:T(1024)} %param.39) | copy-start | bytes 36868
  5.7 68.0 %copy-start.10 = (s32[8192]{0:T(1024)S(1)}, s32[8192]{0:T(1024)}, u32[]{:S(2)}) copy-start(s32[8192]{0:T(1024)} %param.44) | copy-start | bytes 98308
  5.7 68.0 %copy-start.11 = (s32[3072]{0:T(1024)S(1)}, s32[3072]{0:T(1024)}, u32[]{:S(2)}) copy-start(s32[3072]{0:T(1024)} %param.43) | copy-start | bytes 36868
  5.7 68.0 %copy-start.12 = (s32[3072]{0:T(1024)S(1)}, s32[3072]{0:T(1024)}, u32[]{:S(2)}) copy-start(s32[3072]{0:T(1024)} %param.40) | copy-start | bytes 36868
  5.7 68.0 %copy-start.13 = (s32[3072]{0:T(1024)S(1)}, s32[3072]{0:T(1024)}, u32[]{:S(2)}) copy-start(s32[3072]{0:T(1024)} %param.42) | copy-start | bytes 36868
  5.8 68.0 %copy-start.15 = (s32[512]{0:T(512)S(1)}, s32[512]{0:T(512)}, u32[]{:S(2)}) copy-start(s32[512]{0:T(512)} %param.38) | copy-start | bytes 6148
  74.2 0.8 %copy-start.16 = (f32[3,2]{0,1:T(2,128)}, f32[3,2]{0,1:T(2,128)S(1)}, u32[]{:S(2)}) copy-start(f32[3,2]{0,1:T(2,128)S(1)} %get-tuple-element.810) | copy-start | bytes 76

commit v2 on v1

--- a/solution.py
+++ b/solution.py
@@ -688,8 +688,12 @@
     turns = [
         lax.rem(place - lax.rem(jnp.maximum(most, 0), LD) + LD, LD).astype(F32) for most, _, _ in channel
     ]
+    ahead = [
+        jnp.where(most >= 0, lax.rem(jnp.maximum(most, 0) % LD - place + LD, LD), -1).astype(F32)
+        for most, _, _ in channel
+    ]
     flags = jnp.where(row == 0, faults, jnp.where(row == 1, turns[1], turns[0]))
-    flag_ref[...] = flags
+    flag_ref[...] = jnp.where(row == 3, ahead[0], jnp.where(row == 4, ahead[1], flags))
 
 
 def stack2(value):
@@ -721,14 +725,14 @@
     trace_high, trace_low, stiff_high, stiff_low, lift_high, lift_low, onto_ref, own_ref, near_ref, far_ref,
     x_out, norm_out,
     dirn, volume, traces, pairs, faces, scatter, gather, gather_chan, gather_lat, send_chan, send_lat,
-    far_rows, coefs, snd_chan, snd_lat, rcv_chan, rcv_lat, sums, landing,
-    send_sem, recv_sem, sum_send, sum_recv,
+    far_rows, coefs, snd_chan, snd_lat, snd_pass, kept_pass, rcv_chan, rcv_lat, rcv_pass, turns, sums, landing,
+    send_sem, recv_sem, turn_send, turn_recv, sum_send, sum_recv,
 ):
     count = lax.axis_size(axis)
     me = lax.axis_index(axis)
     group, place = me // LD, lax.rem(me, LD)
     groups = count // LD
-    slots = x_ref.shape[1]
+    slots, half = x_ref.shape[1], capacity // 2
     mesh_id = pl.DeviceIdType.MESH
     barrier = pltpu.get_barrier_semaphore()
 
@@ -755,6 +759,27 @@
             gather_chan[d] = hot(iota((capacity, capacity), 0) == line[:, :capacity])
         else:
             gather_lat[d - 2] = hot(iota((LD * LATERAL, LATERAL), 0) == line[:, :LATERAL])
+    size, inv = elem_ref[0:1], elem_ref[1:2]
+    pl.semaphore_wait(barrier, count - 1)
+
+    def across(side, turn):
+        other = lax.rem(group + (1 if side == 0 else groups - 1), groups)
+        return (other * LD + lax.rem(place + turn, LD),)
+
+    told = [
+        pltpu.make_async_remote_copy(
+            src_ref=flag_ref,
+            dst_ref=turns.at[side, turn],
+            send_sem=turn_send.at[side * LD + turn],
+            recv_sem=turn_recv.at[side * LD + turn],
+            device_id=across(side, turn),
+            device_id_type=mesh_id,
+        )
+        for side in range(2)
+        for turn in range(LD)
+    ]
+    for copy in told:
+        copy.start()
     send_elem = send_ref[0:1]
     send_chan[0] = hot(iota((slots, capacity), 0) == send_elem[:, :capacity])
     send_chan[1] = hot(iota((slots, capacity), 0) == send_elem[:, capacity : 2 * capacity])
@@ -789,8 +814,8 @@
         iota(sums.shape, 1) == 0, 1.0, 0.0
     )
 
-    size, inv = elem_ref[0:1], elem_ref[1:2]
-    pl.semaphore_wait(barrier, count - 1)
+    for copy in told:
+        copy.wait()
 
     def step(it, carry):
         field = x_out[...]
@@ -807,41 +832,47 @@
         outgoing = jnp.concatenate(
             [fold_pair(dot(pairs[1], send_chan[0])), fold_pair(dot(pairs[0], send_chan[1])), lateral], axis=1
         )
-        outgoing = choose(dot(onto_ref[...], stack3(outgoing)), 72, send_ref[2:3])
-        snd_chan[0] = outgoing[:, :capacity]
-        snd_chan[1] = outgoing[:, capacity : 2 * capacity]
+        outgoing = choose(dot(onto_ref[...], stack3(outgoing)), 80, send_ref[2:3])
+        for side in range(2):
+            for turn in range(LD):
+                low, left = 40 * (turn // 2), side * capacity + half * (turn % 2)
+                snd_chan[side, turn] = outgoing[low : low + 40, left : left + half]
         for pos in range(LD - 1):
             start = 2 * capacity + pos * LATERAL
             snd_lat[pos] = outgoing[:, start : start + LATERAL]
 
-        copies = []
-        for side in range(2):
-            other = lax.rem(group + (1 if side == 0 else groups - 1), groups)
-            for turn in range(LD):
-                k = side * LD + turn
-                copies.append(
-                    pltpu.make_async_remote_copy(
-                        src_ref=snd_chan.at[side],
-                        dst_ref=rcv_chan.at[it, side, turn],
-                        send_sem=send_sem.at[it, k],
-                        recv_sem=recv_sem.at[it, k],
-                        device_id=(other * LD + lax.rem(place + turn, LD),),
-                        device_id_type=mesh_id,
-                    )
-                )
-        for pos in range(LD - 1):
-            k = 2 * LD + pos
-            copies.append(
-                pltpu.make_async_remote_copy(
-                    src_ref=snd_lat.at[pos],
-                    dst_ref=rcv_lat.at[it, pos],
-                    send_sem=send_sem.at[it, k],
-                    recv_sem=recv_sem.at[it, k],
-                    device_id=(group * LD + lax.rem(place + pos + 1, LD),),
-                    device_id_type=mesh_id,
-                )
+        def send(source, target, k, place_of):
+            return pltpu.make_async_remote_copy(
+                src_ref=source,
+                dst_ref=target,
+                send_sem=send_sem.at[it, k],
+                recv_sem=recv_sem.at[it, k],
+                device_id=place_of,
+                device_id_type=mesh_id,
             )
-        for copy in copies:
+
+        def beside(turn):
+            return (group * LD + lax.rem(place + turn, LD),)
+
+        pairs_of = [(side, turn) for side in range(2) for turn in range(LD)]
+        channel = [
+            send(snd_chan.at[side, turn], rcv_chan.at[it, side, turn], side * LD + turn, across(side, turn))
+            for side, turn in pairs_of
+        ]
+        lateral = [
+            send(snd_lat.at[pos], rcv_lat.at[it, pos], 2 * LD + pos, beside(pos + 1)) for pos in range(LD - 1)
+        ]
+        passed = [
+            send(
+                snd_pass.at[side, turn - 1],
+                rcv_pass.at[it, side, turn - 1],
+                (3 + side) * LD + turn - 1,
+                beside(turn),
+            )
+            for side, turn in pairs_of
+            if turn
+        ]
+        for copy in channel + lateral:
             copy.start()
 
         volume[...] = dot3(stiff_high[...], stiff_low[...], field) * size
@@ -865,18 +896,40 @@
             faces[pl.ds(pl.multiple_of(80 * d, 8), 80)] = back + jnp.concatenate([value, slope], axis=0)
             return inner
 
-        lax.fori_loop(0, 6, local_faces, 0)
-        for copy in copies:
+        lax.fori_loop(0, 4, local_faces, 0)
+        for copy in channel:
+            copy.wait()
+        for side in range(2):
+            for turn in range(LD):
+                chunk = jnp.zeros((40, half), F32)
+                for k in range(LD):
+                    mine = turns[side, k, 3 + side : 4 + side, 0:1] == float((turn + k) % LD)
+                    chunk = jnp.where(mine, rcv_chan[it, side, k], chunk)
+                if turn:
+                    snd_pass[side, turn - 1] = chunk
+                else:
+                    kept_pass[side] = chunk
+        for copy in passed:
+            copy.start()
+        lax.fori_loop(4, 6, local_faces, 0)
+        for copy in passed + lateral:
             copy.wait()
 
         pieces = []
         for side in range(2):
             turn = flag_ref[side + 1 : side + 2, 0:1]
-            got = rcv_chan[it, side, 0]
-            for k in range(1, LD):
-                got = jnp.where(turn == float(k), rcv_chan[it, side, k], got)
+            landed = [kept_pass[side]] + [rcv_pass[it, side, k] for k in range(LD - 1)]
+            chunks = []
+            for k in range(LD):
+                chunk = landed[(-k) % LD]
+                for t in range(1, LD):
+                    chunk = jnp.where(turn == float(t), landed[(t - k) % LD], chunk)
+                chunks.append(chunk)
+            got = jnp.concatenate(
+                [jnp.concatenate(chunks[:2], axis=1), jnp.concatenate(chunks[2:], axis=1)], axis=0
+            )
             pieces.append(fold_pair(dot(stack2(got), gather_chan[side])))
-        sides = [rcv_lat[it, pos] for pos in range(LD - 1)] + [jnp.zeros((72, LATERAL), F32)]
+        sides = [rcv_lat[it, pos] for pos in range(LD - 1)] + [jnp.zeros((80, LATERAL), F32)]
         got = stack2(jnp.concatenate(sides, axis=1))
         for d in range(4):
             pieces.append(fold_pair(dot(got, gather_lat[d])))
@@ -993,11 +1046,12 @@
     weight = np.concatenate([face_weight, face_weight], axis=0)
     quarters = [interp[72 * s : 72 * s + 72] for s in range(4)]
     eye = np.eye(72)
-    onto = three(np.concatenate(quarters + [eye], axis=0))
+    onto = three(wide_rows(quarters + [eye]))
     own = three(wide_rows([j.T @ (weight * j) for j in quarters] + [weight * eye]))
     back = [j.T * weight.T for j in quarters]
     near = three(wide_rows(back + [weight * j for j in quarters] + [weight * eye]))
-    far = three(wide_rows(back + [weight * eye]))
+    far = wide_rows(back + [weight * eye])
+    far = three(wide_rows([far.T]).T)
     trace_high, trace_low = split_np(traces)
     stiff_high, stiff_low = split_np(stiffness)
     lift = np.zeros((216, 480))
@@ -1009,7 +1063,7 @@
     constants = (
         prec, trace_high, trace_low, stiff_high, stiff_low, lift_high, lift_low, onto, own, near, far
     )
-    copies = 2 * LD + LD - 1
+    copies, half = 5 * LD, capacity // 2
     x, shown = pl.pallas_call(
         functools.partial(main_kernel, "parts", ITERS, capacity),
         in_specs=[vmem] * 2 + [pl.BlockSpec(memory_space=pltpu.SMEM)] + [vmem] * 16,
@@ -1029,14 +1083,20 @@
             pltpu.VMEM((slots, LD * LATERAL), BF16),
             pltpu.VMEM((8, 2 * capacity + 4 * LATERAL), F32),
             pltpu.VMEM((16, 128), F32),
-            pltpu.VMEM((2, 72, capacity), F32),
-            pltpu.VMEM((LD - 1, 72, LATERAL), F32),
-            pltpu.VMEM((ITERS, 2, LD, 72, capacity), F32),
-            pltpu.VMEM((ITERS, LD - 1, 72, LATERAL), F32),
+            pltpu.VMEM((2, LD, 40, half), F32),
+            pltpu.VMEM((LD - 1, 80, LATERAL), F32),
+            pltpu.VMEM((2, LD - 1, 40, half), F32),
+            pltpu.VMEM((2, 40, half), F32),
+            pltpu.VMEM((ITERS, 2, LD, 40, half), F32),
+            pltpu.VMEM((ITERS, LD - 1, 80, LATERAL), F32),
+            pltpu.VMEM((ITERS, 2, LD - 1, 40, half), F32),
+            pltpu.VMEM((2, LD, 8, 128), F32),
             pltpu.VMEM((8, 128), F32),
             pltpu.VMEM((part_count, 8, 128), F32),
             pltpu.SemaphoreType.DMA((ITERS, copies)),
             pltpu.SemaphoreType.DMA((ITERS, copies)),
+            pltpu.SemaphoreType.DMA((2 * LD,)),
+            pltpu.SemaphoreType.DMA((2 * LD,)),
             pltpu.SemaphoreType.DMA((part_count,)),
             pltpu.SemaphoreType.DMA((part_count,)),
         ],
@@ -1054,7 +1114,7 @@
     rhs, send_rec, rec_elem = arguments[0], arguments[9], arguments[4]
     part_count = lax.axis_size("parts")
     capacity, slots = send_rec.shape[0] // part_count, rhs.shape[1]
-    suits = slots % 128 == 0 and rec_elem.shape[0] % 1024 == 0 and capacity % 128 == 0
+    suits = slots % 128 == 0 and rec_elem.shape[0] % 1024 == 0 and capacity % 256 == 0
     suits = suits and capacity <= slots <= 4096 and part_count % LD == 0 and part_count >= 3 * LD
     if not suits:
         return general_path(*arguments)

time: 75.3 us -> 63.5 us (0.84)
  Pallas kernels: 70.1 us -> 58.3 us
    pallas_call x1, Pallas kernels: 66.7 us -> 54.9 us  [fast_path(): pl.pallas_call(functools.partial(main_kernel, 'parts', ITERS, capacity),...]
where the time goes in v2:
time: 63.5 us; the launch traced here: 63.2 us
  Pallas kernels  58.3 us (92%)
  local copies, waits for them, and re-layouts  2.67 us (4%)
  between operations  2.12 us (3%)
    pallas_call x1, Pallas kernels, fast_path(): pl.pallas_call(functools.partial(main_kernel, 'parts', ITERS, capacity),...  54.9 us
    pallas_call x1, Pallas kernels, set_up(): pl.pallas_call(functools.partial(setup_kernel, 'parts', capacity), in_spe...  3.35 us
    unnamed x24, local copies, waits for them, and re-layouts  1.85 us

profile of v2, /device:TPU:0, one launch (start us, length us, event | category | flops | bytes accessed | tf_op | source)
XLA Modules:
  0.0 63.2 jit_solution(16367138182273374807)
XLA Ops:
  0.6 1.0 %copy.77.x_ref = f32[216,512]{1,0:T(8,128)S(1)} copy(f32[216,512]{1,0:T(8,128)} %param.36) | data formatting | bytes 884736
  1.6 3.3 %set_up.1 = (f32[136,512]{1,0:T(8,128)}, s32[128,128]{1,0:T(8,128)}, s32[8,1024]{1,0:T(8,128)}, f32[8,128]{1,0:T(8,128)}, f32[8,512]{1,0:T(8,128)}) custom-call(s32[4,128]{1,0:T(4,128)} %bitcast.87, s32[24,128]{1,0:T(8,128)} %bitcast.69, s32[24,128]{1,0:T(8,128)} %bitcast.77, s32[24,128]{1,0:T(8,128)} %bitcast.66, s32[24,128]{1,0:T(8,128)} %bitcast.80, ...), custom_call_target="tpu_custom_call" | custom-call | tf_op jit(solution)/shard_map/set_up/pallas_call | solution.py:1019
  5.6 0.0 copy-start
  5.7 0.0 copy-start.2
  5.7 0.0 copy-start.5
  5.7 0.0 copy-start.8
  5.7 0.0 copy-start.9
  5.7 0.0 copy-start.10
  5.7 0.0 copy-start.11
  5.7 0.0 copy-start.12
  5.7 0.0 copy-start.13
  5.8 0.0 copy-start.15
  5.8 54.9 %smooth.1 = (f32[216,512]{1,0:T(8,128)S(1)}, f32[8,128]{1,0:T(8,128)S(1)}) custom-call(f32[216,512]{1,0:T(8,128)S(1)} %copy.77.x_ref, f32[216,512]{1,0:T(8,128)} %rhs_ref.1, f32[1]{0:T(128)S(6)} %copy.76.top_ref, f32[136,512]{1,0:T(8,128)} %get-tuple-element.403.rows_ref, s32[128,128]{1,0:T(8,128)} %get-tuple-element.404.col_ref, ...), custom_call_target="tpu_custom_call" | custom-call | tf_op jit(solution)/shard_map/smooth/pallas_call | solution.py:1067
  60.7 0.5 slice.60
  61.9 0.0 copy-done
  61.9 0.0 copy-done.2
  61.9 0.0 copy-done.5
  61.9 0.0 copy-done.8
  61.9 0.0 copy-done.9
  61.9 0.0 copy-done.10
  61.9 0.0 copy-done.11
  62.0 0.0 copy-done.12
  62.0 0.0 copy-done.13
  62.0 0.0 copy-done.15
  62.0 0.4 conditional.1
  62.0 0.1 copy.49
  62.1 0.1 reshape_squeeze.3
  62.2 0.1 copy.51
  62.4 0.0 copy-start.16
  62.4 0.8 %copy.81 = f32[216,512]{1,0:T(8,128)} copy(f32[216,512]{1,0:T(8,128)S(1)} %get-tuple-element.809) | data formatting | bytes 884736
  63.2 0.0 copy-done.16
  (1 shorter events, 0.0 us)
Async XLA Ops:
  5.6 56.2 %copy-start = (f32[216,512]{1,0:T(8,128)S(1)}, f32[216,512]{1,0:T(8,128)}, u32[]{:S(2)}) copy-start(f32[216,512]{1,0:T(8,128)} %rhs_ref.1) | copy-start | bytes 1327108
  5.7 56.2 %copy-start.2 = (bf16[432,216]{1,0:T(8,128)(2,1)S(1)}, bf16[432,216]{1,0:T(8,128)(2,1)}, u32[]{:S(2)}) copy-start(bf16[432,216]{1,0:T(8,128)(2,1)} %constant.190.clone.trace_high) | copy-start | bytes 559876
  5.7 56.2 %copy-start.5 = (f32[216,1]{1,0:T(8,128)S(1)}, f32[216,1]{1,0:T(8,128)}, u32[]{:S(2)}) copy-start(f32[216,1]{1,0:T(8,128)} %constant.189.clone.prec_ref) | copy-start | bytes 2596
  5.7 56.2 %copy-start.8 = (s32[3072]{0:T(1024)S(1)}, s32[3072]{0:T(1024)}, u32[]{:S(2)}) copy-start(s32[3072]{0:T(1024)} %param.41) | copy-start | bytes 36868
  5.7 56.2 %copy-start.9 = (s32[3072]{0:T(1024)S(1)}, s32[3072]{0:T(1024)}, u32[]{:S(2)}) copy-start(s32[3072]{0:T(1024)} %param.39) | copy-start | bytes 36868
  5.7 56.2 %copy-start.10 = (s32[8192]{0:T(1024)S(1)}, s32[8192]{0:T(1024)}, u32[]{:S(2)}) copy-start(s32[8192]{0:T(1024)} %param.44) | copy-start | bytes 98308
  5.7 56.2 %copy-start.11 = (s32[3072]{0:T(1024)S(1)}, s32[3072]{0:T(1024)}, u32[]{:S(2)}) copy-start(s32[3072]{0:T(1024)} %param.43) | copy-start | bytes 36868
  5.7 56.2 %copy-start.12 = (s32[3072]{0:T(1024)S(1)}, s32[3072]{0:T(1024)}, u32[]{:S(2)}) copy-start(s32[3072]{0:T(1024)} %param.40) | copy-start | bytes 36868
  5.7 56.2 %copy-start.13 = (s32[3072]{0:T(1024)S(1)}, s32[3072]{0:T(1024)}, u32[]{:S(2)}) copy-start(s32[3072]{0:T(1024)} %param.42) | copy-start | bytes 36868
  5.8 56.2 %copy-start.15 = (s32[512]{0:T(512)S(1)}, s32[512]{0:T(512)}, u32[]{:S(2)}) copy-start(s32[512]{0:T(512)} %param.38) | copy-start | bytes 6148
  62.4 0.8 %copy-start.16 = (f32[3,2]{0,1:T(2,128)}, f32[3,2]{0,1:T(2,128)S(1)}, u32[]{:S(2)}) copy-start(f32[3,2]{0,1:T(2,128)S(1)} %get-tuple-element.810) | copy-start | bytes 76

commit v3 on v2

--- a/solution.py
+++ b/solution.py
@@ -721,12 +721,15 @@
 
 def main_kernel(
     axis, iters, capacity,
-    x_ref, rhs_ref, top_ref, rows_ref, col_ref, send_ref, flag_ref, elem_ref, prec_ref,
-    trace_high, trace_low, stiff_high, stiff_low, lift_high, lift_low, onto_ref, own_ref, near_ref, far_ref,
+    x_ref, rhs_hbm, top_ref, rows_ref, col_ref, send_ref, flag_ref, elem_ref, prec_ref,
+    trace_high_hbm, trace_low_hbm, stiff_high_hbm, stiff_low_hbm, lift_high_hbm, lift_low_hbm,
+    onto_hbm, own_hbm, near_hbm, far_hbm,
     x_out, norm_out,
+    rhs_ref, trace_high, trace_low, stiff_high, stiff_low, lift_high, lift_low,
+    onto_ref, own_ref, near_ref, far_ref, load_sem,
     dirn, volume, traces, pairs, faces, scatter, gather, gather_chan, gather_lat, send_chan, send_lat,
-    far_rows, coefs, snd_chan, snd_lat, snd_pass, kept_pass, rcv_chan, rcv_lat, rcv_pass, turns, sums, landing,
-    send_sem, recv_sem, turn_send, turn_recv, sum_send, sum_recv,
+    far_rows, coefs, snd_chan, snd_lat, snd_pass, kept_pass, rcv_chan, rcv_lat, rcv_pass, sums, landing,
+    send_sem, recv_sem, sum_send, sum_recv,
 ):
     count = lax.axis_size(axis)
     me = lax.axis_index(axis)
@@ -742,6 +745,23 @@
         return carry
 
     lax.fori_loop(1, count, greet, 0)
+    held = [
+        (x_ref, x_out),
+        (trace_high_hbm, trace_high),
+        (trace_low_hbm, trace_low),
+        (onto_hbm, onto_ref),
+        (stiff_high_hbm, stiff_high),
+        (stiff_low_hbm, stiff_low),
+        (own_hbm, own_ref),
+        (near_hbm, near_ref),
+        (far_hbm, far_ref),
+        (lift_high_hbm, lift_high),
+        (lift_low_hbm, lift_low),
+        (rhs_hbm, rhs_ref),
+    ]
+    loads = [pltpu.make_async_copy(src, dst, load_sem.at[k]) for k, (src, dst) in enumerate(held)]
+    for load in loads:
+        load.start()
 
     def hot(mask):
         return jnp.where(mask, 1.0, 0.0).astype(BF16)
@@ -760,26 +780,10 @@
         else:
             gather_lat[d - 2] = hot(iota((LD * LATERAL, LATERAL), 0) == line[:, :LATERAL])
     size, inv = elem_ref[0:1], elem_ref[1:2]
-    pl.semaphore_wait(barrier, count - 1)
-
     def across(side, turn):
         other = lax.rem(group + (1 if side == 0 else groups - 1), groups)
         return (other * LD + lax.rem(place + turn, LD),)
 
-    told = [
-        pltpu.make_async_remote_copy(
-            src_ref=flag_ref,
-            dst_ref=turns.at[side, turn],
-            send_sem=turn_send.at[side * LD + turn],
-            recv_sem=turn_recv.at[side * LD + turn],
-            device_id=across(side, turn),
-            device_id_type=mesh_id,
-        )
-        for side in range(2)
-        for turn in range(LD)
-    ]
-    for copy in told:
-        copy.start()
     send_elem = send_ref[0:1]
     send_chan[0] = hot(iota((slots, capacity), 0) == send_elem[:, :capacity])
     send_chan[1] = hot(iota((slots, capacity), 0) == send_elem[:, capacity : 2 * capacity])
@@ -808,38 +812,38 @@
         coefs[2 * k : 2 * k + 1] = rho_next * rho
         coefs[2 * k + 1 : 2 * k + 2] = 2.0 * rho_next / radius
         rho = rho_next
-    x_out[...] = x_ref[...]
     dirn[...] = jnp.zeros_like(dirn)
     sums[...] = jnp.where(iota(sums.shape, 0) == 2 * iters, flag_ref[0:1], 0.0) * jnp.where(
         iota(sums.shape, 1) == 0, 1.0, 0.0
     )
 
-    for copy in told:
-        copy.wait()
+    for load in loads:
+        load.wait()
+    pl.semaphore_wait(barrier, count - 1)
 
     def step(it, carry):
         field = x_out[...]
-        raw = dot3(trace_high[...], trace_low[...], field)
-        raw = jnp.where(lax.rem(iota(raw.shape, 0), 72) >= 36, raw * inv, raw)
-        traces[...] = raw
-        for d in range(6):
-            pairs[d] = stack2(raw[72 * d : 72 * d + 72])
-
-        send_dir = send_ref[1:2, 2 * capacity :]
-        lateral = jnp.zeros((72, LD * LATERAL), F32)
-        for d in range(2, 6):
-            lateral = jnp.where(send_dir == d, fold_pair(dot(pairs[d], send_lat[...])), lateral)
+        field_high, field_low = split(field)
+
+        def trace(first, last):
+            high, low = trace_high[first:last], trace_low[first:last]
+            raw = dot(high, field_high) + (dot(high, field_low) + dot(low, field_high))
+            raw = jnp.where(lax.rem(iota(raw.shape, 0), 72) >= 36, raw * inv, raw)
+            traces[first:last] = raw
+            for d in range(first // 72, last // 72):
+                pairs[d] = stack2(raw[72 * d - first : 72 * d + 72 - first])
+
+        trace(0, 144)
         outgoing = jnp.concatenate(
-            [fold_pair(dot(pairs[1], send_chan[0])), fold_pair(dot(pairs[0], send_chan[1])), lateral], axis=1
+            [fold_pair(dot(pairs[1], send_chan[0])), fold_pair(dot(pairs[0], send_chan[1]))], axis=1
         )
-        outgoing = choose(dot(onto_ref[...], stack3(outgoing)), 80, send_ref[2:3])
+        outgoing = choose(dot(onto_ref[...], stack3(outgoing)), 80, send_ref[2:3, : 2 * capacity])
+        spare = iota((40, half), 0) >= 36
         for side in range(2):
+            ahead = flag_ref[3 + side : 4 + side, 0:1]
             for turn in range(LD):
                 low, left = 40 * (turn // 2), side * capacity + half * (turn % 2)
-                snd_chan[side, turn] = outgoing[low : low + 40, left : left + half]
-        for pos in range(LD - 1):
-            start = 2 * capacity + pos * LATERAL
-            snd_lat[pos] = outgoing[:, start : start + LATERAL]
+                snd_chan[side, turn] = jnp.where(spare, ahead, outgoing[low : low + 40, left : left + half])
 
         def send(source, target, k, place_of):
             return pltpu.make_async_remote_copy(
@@ -872,7 +876,18 @@
             for side, turn in pairs_of
             if turn
         ]
-        for copy in channel + lateral:
+        for copy in channel:
+            copy.start()
+
+        trace(144, 432)
+        send_dir = send_ref[1:2, 2 * capacity :]
+        outgoing = jnp.zeros((72, LD * LATERAL), F32)
+        for d in range(2, 6):
+            outgoing = jnp.where(send_dir == d, fold_pair(dot(pairs[d], send_lat[...])), outgoing)
+        outgoing = choose(dot(onto_ref[...], stack3(outgoing)), 80, send_ref[2:3, 2 * capacity :])
+        for pos in range(LD - 1):
+            snd_lat[pos] = outgoing[:, pos * LATERAL : (pos + 1) * LATERAL]
+        for copy in lateral:
             copy.start()
 
         volume[...] = dot3(stiff_high[...], stiff_low[...], field) * size
@@ -896,14 +911,14 @@
             faces[pl.ds(pl.multiple_of(80 * d, 8), 80)] = back + jnp.concatenate([value, slope], axis=0)
             return inner
 
-        lax.fori_loop(0, 4, local_faces, 0)
+        lax.fori_loop(2, 6, local_faces, 0)
         for copy in channel:
             copy.wait()
         for side in range(2):
             for turn in range(LD):
                 chunk = jnp.zeros((40, half), F32)
                 for k in range(LD):
-                    mine = turns[side, k, 3 + side : 4 + side, 0:1] == float((turn + k) % LD)
+                    mine = rcv_chan[it, side, k][36:37, 0:1] == float((turn + k) % LD)
                     chunk = jnp.where(mine, rcv_chan[it, side, k], chunk)
                 if turn:
                     snd_pass[side, turn - 1] = chunk
@@ -911,8 +926,37 @@
                     kept_pass[side] = chunk
         for copy in passed:
             copy.start()
-        lax.fori_loop(4, 6, local_faces, 0)
-        for copy in passed + lateral:
+        lax.fori_loop(0, 2, local_faces, 0)
+        for copy in lateral:
+            copy.wait()
+
+        def add_far(pieces, first, last, width):
+            found = jnp.concatenate(pieces, axis=1)
+            left = first * capacity if first < 2 else 2 * capacity
+            part = slice(left, left + width * (last - first))
+            found = choose(dot(far_ref[...], stack3(found)), 80, far_rows[0:1, part].astype(jnp.int32))
+            jump, flux = far_rows[1:2, part], far_rows[2:3, part]
+            terms = stack2(
+                jnp.concatenate([flux * found[40:] - jump * found[:40], flux * found[:40]], axis=0)
+            )
+            for d in range(first, last):
+                start = (d - first) * width
+                faces[80 * d : 80 * d + 80] += fold_pair(
+                    dot(terms[:, start : start + width], scatter[d, :width])
+                )
+
+        def lifted(first, last):
+            total = faces[80 * first : 80 * last]
+            total = jnp.where(lax.rem(iota(total.shape, 0), 80) >= 40, total * inv, total)
+            high, low = split(total)
+            left, rest = lift_high[:, 80 * first : 80 * last], lift_low[:, 80 * first : 80 * last]
+            return dot(left, high) + (dot(left, low) + dot(rest, high))
+
+        sides = [rcv_lat[it, pos] for pos in range(LD - 1)] + [jnp.zeros((80, LATERAL), F32)]
+        got = stack2(jnp.concatenate(sides, axis=1))
+        add_far([fold_pair(dot(got, gather_lat[d])) for d in range(4)], 2, 6, LATERAL)
+        volume[...] += lifted(2, 6)
+        for copy in passed:
             copy.wait()
 
         pieces = []
@@ -929,25 +973,8 @@
                 [jnp.concatenate(chunks[:2], axis=1), jnp.concatenate(chunks[2:], axis=1)], axis=0
             )
             pieces.append(fold_pair(dot(stack2(got), gather_chan[side])))
-        sides = [rcv_lat[it, pos] for pos in range(LD - 1)] + [jnp.zeros((80, LATERAL), F32)]
-        got = stack2(jnp.concatenate(sides, axis=1))
-        for d in range(4):
-            pieces.append(fold_pair(dot(got, gather_lat[d])))
-        found = jnp.concatenate(pieces, axis=1)
-        found = choose(dot(far_ref[...], stack3(found)), 80, far_rows[0:1].astype(jnp.int32))
-        jump, flux = far_rows[1:2], far_rows[2:3]
-        terms = stack2(
-            jnp.concatenate([flux * found[40:] - jump * found[:40], flux * found[:40]], axis=0)
-        )
-        for d in range(6):
-            width = capacity if d < 2 else LATERAL
-            start = d * capacity if d < 2 else 2 * capacity + (d - 2) * LATERAL
-            faces[80 * d : 80 * d + 80] += fold_pair(
-                dot(terms[:, start : start + width], scatter[d, :width])
-            )
-        total = faces[...]
-        total = jnp.where(lax.rem(iota(total.shape, 0), 80) >= 40, total * inv, total)
-        applied = volume[...] + dot3(lift_high[...], lift_low[...], total)
+        add_far(pieces, 0, 2, capacity)
+        applied = volume[...] + lifted(0, 2)
         residual = jnp.where(size > 0.0, rhs_ref[...] - applied, 0.0)
         scaled = residual * (inv * prec_ref[...])
         first = coefs[pl.ds(2 * it, 1), 0:1]
@@ -1064,12 +1091,16 @@
         prec, trace_high, trace_low, stiff_high, stiff_low, lift_high, lift_low, onto, own, near, far
     )
     copies, half = 5 * LD, capacity // 2
+    hbm = pl.BlockSpec(memory_space=pltpu.HBM)
     x, shown = pl.pallas_call(
         functools.partial(main_kernel, "parts", ITERS, capacity),
-        in_specs=[vmem] * 2 + [pl.BlockSpec(memory_space=pltpu.SMEM)] + [vmem] * 16,
+        in_specs=[hbm] * 2 + [pl.BlockSpec(memory_space=pltpu.SMEM)] + [vmem] * 6 + [hbm] * 10,
         out_specs=[vmem] * 2,
         out_shape=[jax.ShapeDtypeStruct((216, slots), F32), jax.ShapeDtypeStruct((8, 128), F32)],
         scratch_shapes=[
+            pltpu.VMEM((216, slots), F32),
+            *[pltpu.VMEM(array.shape, BF16) for array in constants[1:]],
+            pltpu.SemaphoreType.DMA((12,)),
             pltpu.VMEM((216, slots), F32),
             pltpu.VMEM((216, slots), F32),
             pltpu.VMEM((432, slots), F32),
@@ -1090,13 +1121,10 @@
             pltpu.VMEM((ITERS, 2, LD, 40, half), F32),
             pltpu.VMEM((ITERS, LD - 1, 80, LATERAL), F32),
             pltpu.VMEM((ITERS, 2, LD - 1, 40, half), F32),
-            pltpu.VMEM((2, LD, 8, 128), F32),
             pltpu.VMEM((8, 128), F32),
             pltpu.VMEM((part_count, 8, 128), F32),
             pltpu.SemaphoreType.DMA((ITERS, copies)),
             pltpu.SemaphoreType.DMA((ITERS, copies)),
-            pltpu.SemaphoreType.DMA((2 * LD,)),
-            pltpu.SemaphoreType.DMA((2 * LD,)),
             pltpu.SemaphoreType.DMA((part_count,)),
             pltpu.SemaphoreType.DMA((part_count,)),
         ],

time: 63.5 us -> 56.3 us (0.89)
  Pallas kernels: 58.3 us -> 51.1 us
    pallas_call x1, Pallas kernels: 54.9 us -> 47.8 us  [fast_path(): pl.pallas_call(functools.partial(main_kernel, 'parts', ITERS, capacity),...]
where the time goes in v3:
time: 56.3 us; the launch traced here: 56 us
  Pallas kernels  51.1 us (91%)
  local copies, waits for them, and re-layouts  2.67 us (5%)
  between operations  2.12 us (4%)
    pallas_call x1, Pallas kernels, fast_path(): pl.pallas_call(functools.partial(main_kernel, 'parts', ITERS, capacity),...  47.8 us
    pallas_call x1, Pallas kernels, set_up(): pl.pallas_call(functools.partial(setup_kernel, 'parts', capacity), in_spe...  3.35 us
    unnamed x24, local copies, waits for them, and re-layouts  1.85 us

profile of v3, /device:TPU:0, one launch (start us, length us, event | category | flops | bytes accessed | tf_op | source)
XLA Modules:
  0.0 56.0 jit_solution(8535081985504668081)
XLA Ops:
  0.6 1.0 %copy.77.x_ref = f32[216,512]{1,0:T(8,128)S(1)} copy(f32[216,512]{1,0:T(8,128)} %param.36) | data formatting | bytes 884736
  1.6 3.3 %set_up.1 = (f32[136,512]{1,0:T(8,128)}, s32[128,128]{1,0:T(8,128)}, s32[8,1024]{1,0:T(8,128)}, f32[8,128]{1,0:T(8,128)}, f32[8,512]{1,0:T(8,128)}) custom-call(s32[4,128]{1,0:T(4,128)} %bitcast.87, s32[24,128]{1,0:T(8,128)} %bitcast.69, s32[24,128]{1,0:T(8,128)} %bitcast.77, s32[24,128]{1,0:T(8,128)} %bitcast.66, s32[24,128]{1,0:T(8,128)} %bitcast.80, ...), custom_call_target="tpu_custom_call" | custom-call | tf_op jit(solution)/shard_map/set_up/pallas_call | solution.py:1046
  5.6 0.0 copy-start
  5.7 0.0 copy-start.2
  5.7 0.0 copy-start.5
  5.7 0.0 copy-start.8
  5.7 0.0 copy-start.9
  5.7 0.0 copy-start.10
  5.7 0.0 copy-start.11
  5.7 0.0 copy-start.12
  5.7 0.0 copy-start.13
  5.8 0.0 copy-start.15
  5.8 47.8 %smooth.1 = (f32[216,512]{1,0:T(8,128)S(1)}, f32[8,128]{1,0:T(8,128)S(1)}) custom-call(f32[216,512]{1,0:T(8,128)S(1)} %copy.77.x_ref, f32[216,512]{1,0:T(8,128)} %rhs_hbm.1, f32[1]{0:T(128)S(6)} %copy.76.top_ref, f32[136,512]{1,0:T(8,128)} %get-tuple-element.403.rows_ref, s32[128,128]{1,0:T(8,128)} %get-tuple-element.404.col_ref, ...), custom_call_target="tpu_custom_call" | custom-call | tf_op jit(solution)/shard_map/smooth/pallas_call | solution.py:1095
  53.5 0.5 slice.60
  54.7 0.0 copy-done
  54.7 0.0 copy-done.2
  54.7 0.0 copy-done.5
  54.7 0.0 copy-done.8
  54.7 0.0 copy-done.9
  54.8 0.0 copy-done.10
  54.8 0.0 copy-done.11
  54.8 0.0 copy-done.12
  54.8 0.0 copy-done.13
  54.8 0.0 copy-done.15
  54.8 0.4 conditional.1
  54.8 0.1 copy.49
  54.9 0.1 reshape_squeeze.3
  55.0 0.1 copy.51
  55.2 0.0 copy-start.16
  55.2 0.8 %copy.81 = f32[216,512]{1,0:T(8,128)} copy(f32[216,512]{1,0:T(8,128)S(1)} %get-tuple-element.809) | data formatting | bytes 884736
  56.0 0.0 copy-done.16
  (1 shorter events, 0.0 us)
Async XLA Ops:
  5.6 49.1 %copy-start = (f32[216,512]{1,0:T(8,128)S(1)}, f32[216,512]{1,0:T(8,128)}, u32[]{:S(2)}) copy-start(f32[216,512]{1,0:T(8,128)} %rhs_hbm.1) | copy-start | bytes 1327108
  5.7 49.1 %copy-start.2 = (bf16[432,216]{1,0:T(8,128)(2,1)S(1)}, bf16[432,216]{1,0:T(8,128)(2,1)}, u32[]{:S(2)}) copy-start(bf16[432,216]{1,0:T(8,128)(2,1)} %constant.190.clone.trace_high_hbm) | copy-start | bytes 559876
  5.7 49.1 %copy-start.5 = (f32[216,1]{1,0:T(8,128)S(1)}, f32[216,1]{1,0:T(8,128)}, u32[]{:S(2)}) copy-start(f32[216,1]{1,0:T(8,128)} %constant.189.clone.prec_ref) | copy-start | bytes 2596
  5.7 49.1 %copy-start.8 = (s32[3072]{0:T(1024)S(1)}, s32[3072]{0:T(1024)}, u32[]{:S(2)}) copy-start(s32[3072]{0:T(1024)} %param.41) | copy-start | bytes 36868
  5.7 49.1 %copy-start.9 = (s32[3072]{0:T(1024)S(1)}, s32[3072]{0:T(1024)}, u32[]{:S(2)}) copy-start(s32[3072]{0:T(1024)} %param.39) | copy-start | bytes 36868
  5.7 49.1 %copy-start.10 = (s32[8192]{0:T(1024)S(1)}, s32[8192]{0:T(1024)}, u32[]{:S(2)}) copy-start(s32[8192]{0:T(1024)} %param.44) | copy-start | bytes 98308
  5.7 49.1 %copy-start.11 = (s32[3072]{0:T(1024)S(1)}, s32[3072]{0:T(1024)}, u32[]{:S(2)}) copy-start(s32[3072]{0:T(1024)} %param.43) | copy-start | bytes 36868
  5.7 49.1 %copy-start.12 = (s32[3072]{0:T(1024)S(1)}, s32[3072]{0:T(1024)}, u32[]{:S(2)}) copy-start(s32[3072]{0:T(1024)} %param.40) | copy-start | bytes 36868
  5.7 49.0 %copy-start.13 = (s32[3072]{0:T(1024)S(1)}, s32[3072]{0:T(1024)}, u32[]{:S(2)}) copy-start(s32[3072]{0:T(1024)} %param.42) | copy-start | bytes 36868
  5.8 49.0 %copy-start.15 = (s32[512]{0:T(512)S(1)}, s32[512]{0:T(512)}, u32[]{:S(2)}) copy-start(s32[512]{0:T(512)} %param.38) | copy-start | bytes 6148
  55.2 0.8 %copy-start.16 = (f32[3,2]{0,1:T(2,128)}, f32[3,2]{0,1:T(2,128)S(1)}, u32[]{:S(2)}) copy-start(f32[3,2]{0,1:T(2,128)S(1)} %get-tuple-element.810) | copy-start | bytes 76

commit v4 on v3

--- a/solution.py
+++ b/solution.py
@@ -497,7 +497,7 @@
         coef = lax.dynamic_index_in_dim(coefs, step_index, 0, False)
         return tuple(apply_call(step_index, coef, x, dirn, *moved, sums))
 
-    x, dirn, sums = lax.fori_loop(0, ITERS, one_step, (start, start, jnp.zeros((8, 128), F32)))
+    x, dirn, sums = lax.fori_loop(0, ITERS, one_step, (start + 0.0 * top_value, jnp.zeros_like(start), jnp.zeros((8, 128), F32)))
     norms = 0.5 * jnp.log(all_sums(sums)[: 2 * ITERS, 0].reshape(ITERS, 2) / scale_total)
     return (x, norms)
 
@@ -911,10 +911,9 @@
             faces[pl.ds(pl.multiple_of(80 * d, 8), 80)] = back + jnp.concatenate([value, slope], axis=0)
             return inner
 
-        lax.fori_loop(2, 6, local_faces, 0)
-        for copy in channel:
-            copy.wait()
-        for side in range(2):
+        def pass_on(side):
+            for copy in channel[side * LD : side * LD + LD]:
+                copy.wait()
             for turn in range(LD):
                 chunk = jnp.zeros((40, half), F32)
                 for k in range(LD):
@@ -924,8 +923,12 @@
                     snd_pass[side, turn - 1] = chunk
                 else:
                     kept_pass[side] = chunk
-        for copy in passed:
-            copy.start()
+            for copy in passed[side * (LD - 1) : (side + 1) * (LD - 1)]:
+                copy.start()
+
+        lax.fori_loop(2, 6, local_faces, 0)
+        pass_on(0)
+        pass_on(1)
         lax.fori_loop(0, 2, local_faces, 0)
         for copy in lateral:
             copy.wait()

time: 56.3 us -> 56.6 us (level)
    unnamed x24 -> x27, local copies, waits for them, and re-layouts: 1.85 us -> 1.89 us
where the time goes in v4:
time: 56.6 us; the launch traced here: 56.3 us
  Pallas kernels  51.4 us (91%)
  local copies, waits for them, and re-layouts  2.7 us (5%)
  between operations  2.15 us (4%)
    pallas_call x1, Pallas kernels, fast_path(): pl.pallas_call(functools.partial(main_kernel, 'parts', ITERS, capacity),...  48 us
    pallas_call x1, Pallas kernels, set_up(): pl.pallas_call(functools.partial(setup_kernel, 'parts', capacity), in_spe...  3.37 us
    unnamed x27, local copies, waits for them, and re-layouts  1.89 us

profile of v4, /device:TPU:0, one launch (start us, length us, event | category | flops | bytes accessed | tf_op | source)
XLA Modules:
  0.0 56.3 jit_solution(5302539919535762739)
XLA Ops:
  0.6 3.4 %set_up.1 = (f32[136,512]{1,0:T(8,128)}, s32[128,128]{1,0:T(8,128)}, s32[8,1024]{1,0:T(8,128)}, f32[8,128]{1,0:T(8,128)}, f32[8,512]{1,0:T(8,128)}) custom-call(s32[4,128]{1,0:T(4,128)} %bitcast.87, s32[24,128]{1,0:T(8,128)} %bitcast.69, s32[24,128]{1,0:T(8,128)} %bitcast.77, s32[24,128]{1,0:T(8,128)} %bitcast.66, s32[24,128]{1,0:T(8,128)} %bitcast.80, ...), custom_call_target="tpu_custom_call" | custom-call | tf_op jit(solution)/shard_map/set_up/pallas_call | solution.py:1049
  4.6 0.0 copy-start
  4.7 0.0 copy-start.2
  4.7 0.0 copy-start.3
  4.7 0.0 copy-start.6
  4.7 0.0 copy-start.10
  4.7 0.0 copy-start.12
  4.7 0.0 copy-start.13
  4.7 0.0 copy-start.14
  4.7 0.0 copy-start.15
  4.8 0.0 copy-start.16
  4.8 0.0 copy-start.17
  4.8 0.0 copy-start.19
  4.8 48.0 %smooth.1 = (f32[216,512]{1,0:T(8,128)}, f32[8,128]{1,0:T(8,128)S(1)}) custom-call(f32[216,512]{1,0:T(8,128)} %x_ref.1, f32[216,512]{1,0:T(8,128)} %rhs_hbm.1, f32[1]{0:T(128)S(6)} %copy.76.top_ref, f32[136,512]{1,0:T(8,128)} %get-tuple-element.403.rows_ref, s32[128,128]{1,0:T(8,128)} %get-tuple-element.404.col_ref, s32[8,1024]{1,0:T(8,128)} %get-tuple-element.405.send_ref, ...), custom_call_target="tpu_custom_call" | custom-call | tf_op jit(solution)/shard_map/smooth/pallas_call | solution.py:1098
  52.8 0.5 slice.60
  54.0 0.0 copy-done
  54.0 0.0 copy-done.2
  54.0 0.0 copy-done.3
  54.0 0.0 copy-done.6
  54.0 0.0 copy-done.10
  54.0 0.0 copy-done.12
  54.0 0.0 copy-done.13
  54.1 0.0 copy-done.14
  54.1 0.0 copy-done.15
  54.1 0.0 copy-done.16
  54.1 0.0 copy-done.17
  54.1 0.0 copy-done.19
  54.1 0.4 conditional.1
  54.1 0.1 copy.49
  54.2 0.1 reshape_squeeze.3
  54.3 0.1 copy.51
  54.5 0.0 copy-start.20
  54.5 1.8 %copy.81 = f32[216,512]{1,0:T(8,128)} copy(f32[216,512]{1,0:T(8,128)} %get-tuple-element.809) | data formatting | bytes 884736
  56.3 0.0 copy-done.20
  (1 shorter events, 0.0 us)
Async XLA Ops:
  4.6 49.3 %copy-start = (f32[216,512]{1,0:T(8,128)S(1)}, f32[216,512]{1,0:T(8,128)}, u32[]{:S(2)}) copy-start(f32[216,512]{1,0:T(8,128)} %rhs_hbm.1) | copy-start | bytes 1327108
  4.7 49.3 %copy-start.2 = (bf16[432,216]{1,0:T(8,128)(2,1)S(1)}, bf16[432,216]{1,0:T(8,128)(2,1)}, u32[]{:S(2)}) copy-start(bf16[432,216]{1,0:T(8,128)(2,1)} %constant.191.clone.trace_high_hbm) | copy-start | bytes 559876
  4.7 49.3 %copy-start.3 = (bf16[432,216]{1,0:T(8,128)(2,1)S(1)}, bf16[432,216]{1,0:T(8,128)(2,1)}, u32[]{:S(2)}) copy-start(bf16[432,216]{1,0:T(8,128)(2,1)} %constant.192.clone.trace_low_hbm) | copy-start | bytes 559876
  4.7 49.3 %copy-start.6 = (f32[216,1]{1,0:T(8,128)S(1)}, f32[216,1]{1,0:T(8,128)}, u32[]{:S(2)}) copy-start(f32[216,1]{1,0:T(8,128)} %constant.190.clone.prec_ref) | copy-start | bytes 2596
  4.7 49.3 %copy-start.10 = (f32[216,512]{1,0:T(8,128)S(1)}, f32[216,512]{1,0:T(8,128)}, u32[]{:S(2)}) copy-start(f32[216,512]{1,0:T(8,128)} %x_ref.1) | copy-start | bytes 1327108
  4.7 49.3 %copy-start.12 = (s32[3072]{0:T(1024)S(1)}, s32[3072]{0:T(1024)}, u32[]{:S(2)}) copy-start(s32[3072]{0:T(1024)} %param.41) | copy-start | bytes 36868
  4.7 49.3 %copy-start.13 = (s32[3072]{0:T(1024)S(1)}, s32[3072]{0:T(1024)}, u32[]{:S(2)}) copy-start(s32[3072]{0:T(1024)} %param.39) | copy-start | bytes 36868
  4.7 49.3 %copy-start.14 = (s32[8192]{0:T(1024)S(1)}, s32[8192]{0:T(1024)}, u32[]{:S(2)}) copy-start(s32[8192]{0:T(1024)} %param.44) | copy-start | bytes 98308
  4.7 49.3 %copy-start.15 = (s32[3072]{0:T(1024)S(1)}, s32[3072]{0:T(1024)}, u32[]{:S(2)}) copy-start(s32[3072]{0:T(1024)} %param.43) | copy-start | bytes 36868
  4.8 49.3 %copy-start.16 = (s32[3072]{0:T(1024)S(1)}, s32[3072]{0:T(1024)}, u32[]{:S(2)}) copy-start(s32[3072]{0:T(1024)} %param.40) | copy-start | bytes 36868
  4.8 49.3 %copy-start.17 = (s32[3072]{0:T(1024)S(1)}, s32[3072]{0:T(1024)}, u32[]{:S(2)}) copy-start(s32[3072]{0:T(1024)} %param.42) | copy-start | bytes 36868
  4.8 49.3 %copy-start.19 = (s32[512]{0:T(512)S(1)}, s32[512]{0:T(512)}, u32[]{:S(2)}) copy-start(s32[512]{0:T(512)} %param.38) | copy-start | bytes 6148
  54.5 1.8 %copy-start.20 = (f32[3,2]{0,1:T(2,128)}, f32[3,2]{0,1:T(2,128)S(1)}, u32[]{:S(2)}) copy-start(f32[3,2]{0,1:T(2,128)S(1)} %get-tuple-element.810) | copy-start | bytes 76

commit v5 on v3

--- a/solution.py
+++ b/solution.py
@@ -911,7 +911,10 @@
             faces[pl.ds(pl.multiple_of(80 * d, 8), 80)] = back + jnp.concatenate([value, slope], axis=0)
             return inner
 
-        lax.fori_loop(2, 6, local_faces, 0)
+        def two_faces(k, inner):
+            return local_faces(2 * k + 1, local_faces(2 * k, inner))
+
+        lax.fori_loop(1, 3, two_faces, 0)
         for copy in channel:
             copy.wait()
         for side in range(2):
@@ -926,7 +929,7 @@
                     kept_pass[side] = chunk
         for copy in passed:
             copy.start()
-        lax.fori_loop(0, 2, local_faces, 0)
+        lax.fori_loop(0, 1, two_faces, 0)
         for copy in lateral:
             copy.wait()
 

time: 56.3 us -> 56.2 us (level)
  no operation moved by 1% of the time
where the time goes in v5:
time: 56.2 us; the launch traced here: 55.9 us
  Pallas kernels  51 us (91%)
  local copies, waits for them, and re-layouts  2.67 us (5%)
  between operations  2.12 us (4%)
    pallas_call x1, Pallas kernels, fast_path(): pl.pallas_call(functools.partial(main_kernel, 'parts', ITERS, capacity),...  47.7 us
    pallas_call x1, Pallas kernels, set_up(): pl.pallas_call(functools.partial(setup_kernel, 'parts', capacity), in_spe...  3.35 us
    unnamed x24, local copies, waits for them, and re-layouts  1.85 us

profile of v5, /device:TPU:0, one launch (start us, length us, event | category | flops | bytes accessed | tf_op | source)
XLA Modules:
  0.0 55.9 jit_solution(14312782814895454909)
XLA Ops:
  0.6 1.0 %copy.77.x_ref = f32[216,512]{1,0:T(8,128)S(1)} copy(f32[216,512]{1,0:T(8,128)} %param.36) | data formatting | bytes 884736
  1.6 3.3 %set_up.1 = (f32[136,512]{1,0:T(8,128)}, s32[128,128]{1,0:T(8,128)}, s32[8,1024]{1,0:T(8,128)}, f32[8,128]{1,0:T(8,128)}, f32[8,512]{1,0:T(8,128)}) custom-call(s32[4,128]{1,0:T(4,128)} %bitcast.87, s32[24,128]{1,0:T(8,128)} %bitcast.69, s32[24,128]{1,0:T(8,128)} %bitcast.77, s32[24,128]{1,0:T(8,128)} %bitcast.66, s32[24,128]{1,0:T(8,128)} %bitcast.80, ...), custom_call_target="tpu_custom_call" | custom-call | tf_op jit(solution)/shard_map/set_up/pallas_call | solution.py:1049
  5.6 0.0 copy-start
  5.7 0.0 copy-start.2
  5.7 0.0 copy-start.5
  5.7 0.0 copy-start.8
  5.7 0.0 copy-start.9
  5.7 0.0 copy-start.10
  5.7 0.0 copy-start.11
  5.7 0.0 copy-start.12
  5.7 0.0 copy-start.13
  5.8 0.0 copy-start.15
  5.8 47.7 %smooth.1 = (f32[216,512]{1,0:T(8,128)S(1)}, f32[8,128]{1,0:T(8,128)S(1)}) custom-call(f32[216,512]{1,0:T(8,128)S(1)} %copy.77.x_ref, f32[216,512]{1,0:T(8,128)} %rhs_hbm.1, f32[1]{0:T(128)S(6)} %copy.76.top_ref, f32[136,512]{1,0:T(8,128)} %get-tuple-element.403.rows_ref, s32[128,128]{1,0:T(8,128)} %get-tuple-element.404.col_ref, ...), custom_call_target="tpu_custom_call" | custom-call | tf_op jit(solution)/shard_map/smooth/pallas_call | solution.py:1098
  53.5 0.5 slice.60
  54.6 0.0 copy-done
  54.6 0.0 copy-done.2
  54.6 0.0 copy-done.5
  54.7 0.0 copy-done.8
  54.7 0.0 copy-done.9
  54.7 0.0 copy-done.10
  54.7 0.0 copy-done.11
  54.7 0.0 copy-done.12
  54.7 0.0 copy-done.13
  54.7 0.0 copy-done.15
  54.7 0.4 conditional.1
  54.7 0.1 copy.49
  54.9 0.1 reshape_squeeze.3
  54.9 0.1 copy.51
  55.1 0.0 copy-start.16
  55.2 0.8 %copy.81 = f32[216,512]{1,0:T(8,128)} copy(f32[216,512]{1,0:T(8,128)S(1)} %get-tuple-element.809) | data formatting | bytes 884736
  55.9 0.0 copy-done.16
  (1 shorter events, 0.0 us)
Async XLA Ops:
  5.6 49.0 %copy-start = (f32[216,512]{1,0:T(8,128)S(1)}, f32[216,512]{1,0:T(8,128)}, u32[]{:S(2)}) copy-start(f32[216,512]{1,0:T(8,128)} %rhs_hbm.1) | copy-start | bytes 1327108
  5.7 49.0 %copy-start.2 = (bf16[432,216]{1,0:T(8,128)(2,1)S(1)}, bf16[432,216]{1,0:T(8,128)(2,1)}, u32[]{:S(2)}) copy-start(bf16[432,216]{1,0:T(8,128)(2,1)} %constant.190.clone.trace_high_hbm) | copy-start | bytes 559876
  5.7 49.0 %copy-start.5 = (f32[216,1]{1,0:T(8,128)S(1)}, f32[216,1]{1,0:T(8,128)}, u32[]{:S(2)}) copy-start(f32[216,1]{1,0:T(8,128)} %constant.189.clone.prec_ref) | copy-start | bytes 2596
  5.7 49.0 %copy-start.8 = (s32[3072]{0:T(1024)S(1)}, s32[3072]{0:T(1024)}, u32[]{:S(2)}) copy-start(s32[3072]{0:T(1024)} %param.41) | copy-start | bytes 36868
  5.7 49.0 %copy-start.9 = (s32[3072]{0:T(1024)S(1)}, s32[3072]{0:T(1024)}, u32[]{:S(2)}) copy-start(s32[3072]{0:T(1024)} %param.39) | copy-start | bytes 36868
  5.7 49.0 %copy-start.10 = (s32[8192]{0:T(1024)S(1)}, s32[8192]{0:T(1024)}, u32[]{:S(2)}) copy-start(s32[8192]{0:T(1024)} %param.44) | copy-start | bytes 98308
  5.7 49.0 %copy-start.11 = (s32[3072]{0:T(1024)S(1)}, s32[3072]{0:T(1024)}, u32[]{:S(2)}) copy-start(s32[3072]{0:T(1024)} %param.43) | copy-start | bytes 36868
  5.7 49.0 %copy-start.12 = (s32[3072]{0:T(1024)S(1)}, s32[3072]{0:T(1024)}, u32[]{:S(2)}) copy-start(s32[3072]{0:T(1024)} %param.40) | copy-start | bytes 36868
  5.7 49.0 %copy-start.13 = (s32[3072]{0:T(1024)S(1)}, s32[3072]{0:T(1024)}, u32[]{:S(2)}) copy-start(s32[3072]{0:T(1024)} %param.42) | copy-start | bytes 36868
  5.8 49.0 %copy-start.15 = (s32[512]{0:T(512)S(1)}, s32[512]{0:T(512)}, u32[]{:S(2)}) copy-start(s32[512]{0:T(512)} %param.38) | copy-start | bytes 6148
  55.1 0.8 %copy-start.16 = (f32[3,2]{0,1:T(2,128)}, f32[3,2]{0,1:T(2,128)S(1)}, u32[]{:S(2)}) copy-start(f32[3,2]{0,1:T(2,128)S(1)} %get-tuple-element.810) | copy-start | bytes 76
